TPU v7x, 8 devices: a whole 2x2x1 slice. The times are simulated.
8 devices in a mesh: dp: 1 (over z), tp: 2 (over y), sp: 4 (over x, core).
Axes of the slice: x: 2, y: 2, z: 1, core: 2. Of those that a mesh axis runs over, the one named last changes fastest.
Arguments:
- hidden: bfloat16 [256, 6144], P('dp')
- norm_w: bfloat16 [6144], replicated
- w_q: bfloat16 [6144, 6144], P(None, 'tp')
- b_q: bfloat16 [6144], P('tp')
- w_k: bfloat16 [6144, 256], P(None, 'tp')
- b_k: bfloat16 [256], P('tp')
- w_v: bfloat16 [6144, 256], P(None, 'tp')
- b_v: bfloat16 [256], P('tp')
- w_o: bfloat16 [6144, 6144], P('tp')
- k_cache: bfloat16 [256, 2048, 2, 128], P('dp', 'sp', 'tp')
- v_cache: bfloat16 [256, 2048, 2, 128], P('dp', 'sp', 'tp')
- positions: int32 [256], P('dp')
- seq_lens: int32 [256], P('dp')
Outputs:
- output 1: bfloat16 [256, 6144], P('dp')
- output 2: bfloat16 [256, 2, 128], P('dp', 'tp')
- output 3: bfloat16 [256, 2, 128], P('dp', 'tp')
All inputs are finite; a program needn't handle non-finite values.
Results may differ from a plain program's by a relative error of at most 0.00769785.
Values sent between devices are 32-bit elements.
A program may use at most 1 GiB of HBM per device.

v0:
```python
import jax
import jax.numpy as jnp
from jax import lax
from jax.sharding import PartitionSpec as P

RMS_EPS = 1.5625e-7
ROPE_BASE = 10000.0
NEG_BIG = -1e30


def rms_norm(x_rows, norm_w):
    x_f32 = x_rows.astype(jnp.float32)
    mean_sq = jnp.mean(x_f32 * x_f32, axis=-1, keepdims=True)
    return (x_f32 * lax.rsqrt(mean_sq + RMS_EPS) * norm_w.astype(jnp.float32)).astype(jnp.bfloat16)


def apply_rotary(heads_in, positions):
    rot_dim = heads_in.shape[-1] // 2
    half_rot = rot_dim // 2
    inv_freq = ROPE_BASE ** (-2.0 * jnp.arange(half_rot, dtype=jnp.float32) / rot_dim)
    angles = positions.astype(jnp.float32)[:, None, None] * inv_freq
    cos_t = jnp.cos(angles)
    sin_t = jnp.sin(angles)
    rot_pairs = heads_in[..., :rot_dim].astype(jnp.float32).reshape(heads_in.shape[:-1] + (half_rot, 2))
    even_part = rot_pairs[..., 0]
    odd_part = rot_pairs[..., 1]
    rotated = jnp.stack([even_part * cos_t - odd_part * sin_t, even_part * sin_t + odd_part * cos_t], axis=-1)
    rotated = rotated.reshape(heads_in.shape[:-1] + (rot_dim,)).astype(jnp.bfloat16)
    return jnp.concatenate([rotated, heads_in[..., rot_dim:]], axis=-1)


def project(normed, weight, bias_vec):
    return (jnp.dot(normed, weight, preferred_element_type=jnp.float32) + bias_vec.astype(jnp.float32)).astype(jnp.bfloat16)


def local_partials(q_grp, k_rot, v_new, k_loc, v_loc, seq_lens, shard_idx):
    s_dev = k_loc.shape[1]
    attn_scale = q_grp.shape[-1] ** -0.5
    cache_pos = shard_idx * s_dev + jnp.arange(s_dev, dtype=jnp.int32)
    valid_mask = (cache_pos[None, :] < seq_lens[:, None])[:, None, None, :]
    s_cache = jnp.einsum('bgqd,bsgd->bgqs', q_grp, k_loc, preferred_element_type=jnp.float32) * attn_scale
    s_cache = jnp.where(valid_mask, s_cache, NEG_BIG)
    is_first = shard_idx == 0
    s_new = jnp.einsum('bgqd,bgd->bgq', q_grp, k_rot, preferred_element_type=jnp.float32) * attn_scale
    s_new = jnp.where(is_first, s_new, NEG_BIG)
    m_loc = jnp.maximum(jnp.max(s_cache, axis=-1), s_new)
    p_cache = jnp.where(valid_mask, jnp.exp(s_cache - m_loc[..., None]), 0.0)
    p_new = jnp.where(is_first, jnp.exp(s_new - m_loc), 0.0)
    l_loc = jnp.sum(p_cache, axis=-1) + p_new
    o_loc = jnp.einsum('bgqs,bsgd->bgqd', p_cache.astype(jnp.bfloat16), v_loc, preferred_element_type=jnp.float32)
    o_loc = o_loc + p_new[..., None] * v_new.astype(jnp.float32)[:, :, None, :]
    return m_loc, l_loc, o_loc


def solution(mesh):
    def device_step(hidden, norm_w, w_q, b_q, w_k, b_k, w_v, b_v, w_o, k_cache, v_cache, positions, seq_lens):
        n_rows = hidden.shape[0]
        groups_dev, head_dim = k_cache.shape[2], k_cache.shape[3]
        heads_dev = w_q.shape[1] // head_dim
        per_group = heads_dev // groups_dev
        normed = rms_norm(hidden, norm_w)
        q_rot = apply_rotary(project(normed, w_q, b_q).reshape(n_rows, heads_dev, head_dim), positions)
        k_rot = apply_rotary(project(normed, w_k, b_k).reshape(n_rows, groups_dev, head_dim), positions)
        v_new = project(normed, w_v, b_v).reshape(n_rows, groups_dev, head_dim)
        q_grp = q_rot.reshape(n_rows, groups_dev, per_group, head_dim)
        m_loc, l_loc, o_loc = local_partials(q_grp, k_rot, v_new, k_cache, v_cache, seq_lens, lax.axis_index('sp'))
        m_all = lax.pmax(m_loc, 'sp')
        factor = jnp.exp(m_loc - m_all)
        l_all, o_all = lax.psum((l_loc * factor, o_loc * factor[..., None]), 'sp')
        attn_rows = (o_all / l_all[..., None]).astype(jnp.bfloat16).reshape(n_rows, heads_dev * head_dim)
        proj_sum = lax.psum(jnp.dot(attn_rows, w_o, preferred_element_type=jnp.float32), 'tp')
        y_out = (hidden.astype(jnp.float32) + proj_sum).astype(jnp.bfloat16)
        return y_out, k_rot, v_new

    col_spec = P(None, 'tp')
    vec_spec = P('tp')
    cache_spec = P('dp', 'sp', 'tp', None)
    group_spec = P('dp', 'tp', None)
    in_specs = (P('dp', None), P(None), col_spec, vec_spec, col_spec, vec_spec, col_spec, vec_spec,
                P('tp', None), cache_spec, cache_spec, P('dp'), P('dp'))
    out_specs = (P('dp', None), group_spec, group_spec)
    return jax.shard_map(device_step, mesh=mesh, in_specs=in_specs, out_specs=out_specs, check_vma=False)
```

profile of v0, /device:TPU:0, one launch (start us, length us, event | category | flops | bytes accessed | tf_op | source)
XLA Modules:
  0.0 360.6 jit_solution(15506556007889696234)
XLA Ops:
  7.3 0.8 convert_element_type.71
  8.1 0.9 convert_element_type.75
  9.0 0.7 convert_element_type.69
  9.6 2.6 fusion.8
  12.3 2.8 fusion.27
  15.2 0.2 multiply_cosine_fusion.1
  15.4 0.2 fusion.36
  15.7 0.6 pad_maximum_fusion.2
  16.4 0.1 copy.33
  16.5 18.8 %fusion.17 = bf16[256,3072]{1,0:T(8,128)(2,1)} fusion(bf16[6144,3072]{1,0:T(8,128)(2,1)} %param.15, f32[3072]{0:T(1024)S(1)} %convert_element_type.67, bf16[256,6144]{1,0:T(8,128)(2,1)} %param.13, f32[6144]{0:T(1024)S(1)} %convert_element_type.65, f32[256]{0:T(256)S(1)} %add_rsqrt_fusion), kind=kOutput, calls=%fused_computation.22 | convolution fusion | flops 9671540736 | bytes 42505216 | tf_op jit(solution)/shard_map/dot_general | solution.py:33
  35.3 1.7 copy.25
  37.0 0.2 slice_convert_fusion
  37.2 0.9 copy.26
  38.2 0.3 subtract_convert_fusion
  38.5 0.2 copy.27
  38.7 1.3 pad_maximum_fusion
  40.0 2.0 copy.28
  41.9 0.1 broadcast_compare_fusion
  42.1 0.9 fusion.48
  43.0 24.3 %fusion.4 = (f32[256,24]{1,0:T(8,128)S(1)}, f32[256,24,512]{2,1,0:T(8,128)}) fusion(pred[256,512]{1,0:T(8,128)(4,1)S(1)} %broadcast_compare_fusion, bf16[256,24,128]{2,1,0:T(8,128)(2,1)S(1)} %copy.28, bf16[256,512,1,128]{3,1,2,0:T(8,128)(2,1)} %param.22), kind=kOutput, calls=%fused_computation.6 | convolution fusion | flops 814737408 | bytes 47865856 | tf_op jit(solution)/shard_map/bgqd,bsgd->bgqs/dot_general | solution.py:41
  67.4 15.0 %pmax.7 = f32[256,1,24]{2,0,1:T(8,128)S(1)} all-reduce(f32[256,1,24]{2,0,1:T(8,128)S(1)} %bitcast.53), channel_id=1, replica_groups=mesh['dp'=1,'tp'=2,'sp'=4] {'sp'}, use_global_device_ids=true, to_apply=%region_2.3 | all-reduce | flops 6144 | bytes 49152 | tf_op jit(solution)/shard_map/pmax | solution.py:67
  82.4 10.6 %fusion.5 = f32[256,24]{1,0:T(8,128)S(1)} fusion(f32[256,24,512]{2,1,0:T(8,128)} %get-tuple-element.33, f32[256,24]{1,0:T(8,128)S(1)} %fusion.29, pred[256,512]{1,0:T(8,128)(4,1)S(1)} %broadcast_compare_fusion), kind=kLoop, calls=%fused_computation.10 | loop fusion | flops 15722496 | bytes 12763136 | tf_op jit(solution)/shard_map/reduce_sum | solution.py:49
  93.1 1.7 fusion.47
  94.9 18.7 %multiply_bitcast_fusion = f32[256,1,24,128]{3,2,0,1:T(8,128)} fusion(bf16[256,512,1,128]{3,1,2,0:T(8,128)(2,1)} %param.23, f32[256,24,512]{2,1,0:T(8,128)} %get-tuple-element.33, f32[256,24]{1,0:T(8,128)S(1)} %fusion.29, pred[256,512]{1,0:T(8,128)(4,1)S(1)} %broadcast_compare_fusion, f32[256,24]{1,0:T(8,128)S(1)} %get-tuple-element.21, ...), kind=kOutput, calls=%fused_computation.24 | convolution fusion | flops 823394304 | bytes 49618944 | tf_op jit(solution)/shard_map/bgqs,bsgd->bgqd/dot_general | solution.py:50
  113.7 14.8 %psum.22 = f32[256,24]{1,0:T(8,128)S(1)} all-reduce(f32[256,24]{1,0:T(8,128)S(1)} %get-tuple-element.15), channel_id=1, replica_groups=mesh['dp'=1,'tp'=2,'sp'=4] {'sp'}, use_global_device_ids=true, to_apply=%region_5.6 | all-reduce | flops 6144 | bytes 49152 | tf_op jit(solution)/shard_map/psum | solution.py:69
  128.6 50.0 %all-reduce.3.cloned.1.call-done = f32[256,1,24,128]{3,2,0,1:T(8,128)} async-done(((f32[256,1,24,128]{3,2,0,1:T(8,128)}), f32[256,1,24,128]{3,2,0,1:T(8,128)}) %all-reduce.3.cloned.1.call-update) | async-done | bytes 3145744 | tf_op jit(solution)/shard_map/psum | solution.py:69
  178.6 2.4 divide_convert_fusion
  181.0 18.8 %fusion.22 = f32[256,6144]{1,0:T(8,128)} fusion(bf16[3072,6144]{1,0:T(8,128)(2,1)} %param.21, bf16[32,8,24,128]{3,2,1,0:T(8,128)(2,1)S(1)} %bitcast.55), kind=kOutput, calls=%fused_computation.25 | convolution fusion | flops 9663676416 | bytes 45613056 | tf_op jit(solution)/shard_map/dot_general | solution.py:71
  199.8 0.8 copy-done.4
  200.6 0.7 copy.32
  201.3 146.1 %all-reduce.5.cloned.1.call-done = f32[256,6144]{1,0:T(8,128)} async-done(((f32[256,6144]{1,0:T(8,128)}), f32[256,6144]{1,0:T(8,128)}) %all-reduce.5.cloned.1.call-update) | async-done | bytes 6291472 | tf_op jit(solution)/shard_map/psum | solution.py:71
  347.4 6.3 %fusion.11 = bf16[256,6144]{1,0:T(8,128)(2,1)} fusion(f32[256,6144]{1,0:T(8,128)} %all-reduce.5.cloned.1.call-done, bf16[256,6144]{1,0:T(8,128)(2,1)} %param.13), kind=kLoop, calls=%fused_computation.15 | loop fusion | flops 4718592 | bytes 12582912 | tf_op jit(solution)/shard_map/convert_element_type | solution.py:72
  (37 shorter events, 0.5 us)
Async XLA Ops:
  7.2 85.9 %copy-start = (bf16[6144,128]{1,0:T(8,128)(2,1)S(1)}, bf16[6144,128]{1,0:T(8,128)(2,1)}, u32[]{:S(2)}) copy-start(bf16[6144,128]{1,0:T(8,128)(2,1)} %param.19) | copy-start | bytes 4718596
  7.2 5.1 %copy-start.8 = (bf16[3072]{0:T(1024)(128)(2,1)S(1)}, bf16[3072]{0:T(1024)(128)(2,1)}, u32[]{:S(2)}) copy-start(bf16[3072]{0:T(1024)(128)(2,1)} %param.16) | copy-start | bytes 18436
  7.2 5.1 %copy-start.7 = (bf16[6144]{0:T(1024)(128)(2,1)S(1)}, bf16[6144]{0:T(1024)(128)(2,1)}, u32[]{:S(2)}) copy-start(bf16[6144]{0:T(1024)(128)(2,1)} %param.14) | copy-start | bytes 36868
  7.2 171.4 %all-reduce.3.cloned.1.call-start = ((), (), s32[]{:S(2)}) async-start(), calls=%async_computation | async-start | bytes 6291456 | tf_op jit(solution)/shard_map/psum | solution.py:69
  7.3 5.0 %copy-start.2 = (bf16[256,6144]{1,0:T(8,128)(2,1)S(1)}, bf16[256,6144]{1,0:T(8,128)(2,1)}, u32[]{:S(2)}) copy-start(bf16[256,6144]{1,0:T(8,128)(2,1)} %param.13) | copy-start | bytes 9437188
  12.3 4.2 %copy-start.5 = (f32[6144]{0:T(1024)}, f32[6144]{0:T(1024)S(1)}, u32[]{:S(2)}) copy-start(f32[6144]{0:T(1024)S(1)} %convert_element_type.65) | copy-start | bytes 73732
  38.7 3.3 copy-start.9
  82.4 10.7 %copy-start.3 = (bf16[256,6144]{1,0:T(8,128)(2,1)S(1)}, bf16[256,6144]{1,0:T(8,128)(2,1)}, u32[]{:S(2)}) copy-start(bf16[256,6144]{1,0:T(8,128)(2,1)} %param.13) | copy-start | bytes 9437188
  82.4 10.7 %copy-start.6 = (f32[6144]{0:T(1024)S(1)}, f32[6144]{0:T(1024)}, u32[]{:S(2)}) copy-start(f32[6144]{0:T(1024)} %copy-done.5) | copy-start | bytes 73732
  113.7 233.8 %all-reduce.5.cloned.1.call-start = ((), (), s32[]{:S(2)}) async-start(), calls=%async_computation.1 | async-start | bytes 12582912 | tf_op jit(solution)/shard_map/psum | solution.py:71
  199.8 0.8 copy-start.4
  347.4 6.3 %copy-start.1 = (bf16[6144,128]{1,0:T(8,128)(2,1)S(1)}, bf16[6144,128]{1,0:T(8,128)(2,1)}, u32[]{:S(2)}) copy-start(bf16[6144,128]{1,0:T(8,128)(2,1)} %param.19) | copy-start | bytes 4718596
Sparse Core Ops, SparseCore 0:
  113.8 64.7 all-reduce.2
  199.9 147.4 all-reduce.4
where the time goes:
time: 361 us
  waiting for transfers between devices  196 us (54%)
  matrix products  86.1 us (24%)
  blocking collectives  29.9 us (8%)
  other arithmetic  27.4 us (8%)
  between operations  14.4 us (4%)
  local copies, waits for them, and re-layouts  6.63 us (2%)
    psum x1, waiting for transfers between devices, device_step(): lax.psum(jnp.dot(attn_rows, w_o, preferred_element_type=jnp.float32), 'tp')  146 us
    psum x1, waiting for transfers between devices, device_step(): l_all, o_all = lax.psum((l_loc * factor, o_loc * factor[..., None]), 'sp')  50 us
    dot_general x1, matrix products, local_partials(): jnp.einsum('bgqd,bsgd->bgqs', q_grp, k_loc, preferred_element_type=jnp.fl...  24.3 us
    dot_general x3, matrix products, project(): jnp.dot(normed, weight, preferred_element_type=jnp.float32)  23.3 us
    dot_general x1, matrix products, device_step(): jnp.dot(attn_rows, w_o, preferred_element_type=jnp.float32)  18.8 us
    dot_general x1, matrix products, local_partials(): jnp.einsum('bgqs,bsgd->bgqd', p_cache.astype(jnp.bfloat16), v_loc, prefer...  18.7 us
    pmax x1, blocking collectives, device_step(): m_all = lax.pmax(m_loc, 'sp')  15 us
    psum x1, blocking collectives, device_step(): l_all, o_all = lax.psum((l_loc * factor, o_loc * factor[..., None]), 'sp')  14.8 us
  transfers between devices with their start and end apart: 2, of which 2 were waited for; matrix products, arithmetic and copies ran while one was open for 0% of the time, Pallas kernels for 0%

commit v1 on v0

v1 whole, which is shorter than its diff:
```python
import functools

import jax
import jax.numpy as jnp
from jax import lax
from jax.experimental import pallas as pl
from jax.experimental.pallas import tpu as pltpu
from jax.sharding import PartitionSpec as P

RMS_EPS = 1.5625e-7
ROPE_BASE = 10000.0
LOG2E = 1.4426950408889634
NEG = -3e38
NEG_FLOOR = -1e38
MESH = pl.DeviceIdType.MESH
VMEM_LIMIT = 67_043_328

NC = 2
BR = 8
NB = 4
TN = 512


def rope_tables(positions, head_dim):
    rot_dim = head_dim // 2
    lane = jnp.arange(head_dim, dtype=jnp.int32)
    freq = ROPE_BASE ** (-2.0 * (lane // 2).astype(jnp.float32) / rot_dim)
    freq = jnp.where(lane < rot_dim, freq, 0.0)
    angles = positions.astype(jnp.float32)[:, None] * freq
    sign = jnp.where(lane % 2 == 0, -1.0, 1.0)
    return jnp.cos(angles), jnp.sin(angles) * sign


def rope(x, cos_t, sin_t, even):
    width = x.shape[-1]
    swapped = jnp.where(even, pltpu.roll(x, width - 1, 1), pltpu.roll(x, 1, 1))
    return (x * cos_t + swapped * sin_t).astype(jnp.bfloat16).astype(jnp.float32)


def qkv_kernel(heads, n_tiles, hid_ref, nw_ref, wq_ref, bq_ref, wk_ref, bk_ref, wv_ref, bv_ref, cos_ref, sin_ref,
               q_ref, kf_ref, vf_ref, kb_ref, vb_ref, normed):
    step = pl.program_id(0)
    n_rows, head_dim = cos_ref.shape

    @pl.when(step == 0)
    def _():
        def norm_rows(i, _):
            rows = pl.ds(pl.multiple_of(i * 32, 32), 32)
            x = hid_ref[rows, :].astype(jnp.float32)
            mean_sq = jnp.mean(x * x, axis=-1, keepdims=True)
            y = x * lax.rsqrt(mean_sq + RMS_EPS) * nw_ref[...].astype(jnp.float32)
            normed[rows, :] = y.astype(jnp.bfloat16)
            return 0
        lax.fori_loop(0, n_rows // 32, norm_rows, 0)

    def even_lanes():
        return lax.broadcasted_iota(jnp.int32, (n_rows, head_dim), 1) % 2 == 0

    def proj(w_ref, b_ref):
        acc = jnp.dot(normed[...], w_ref[...], preferred_element_type=jnp.float32)
        return (acc + b_ref[...].astype(jnp.float32)).astype(jnp.bfloat16).astype(jnp.float32)

    @pl.when(step < n_tiles)
    def _():
        val = proj(wq_ref, bq_ref)
        per_tile = heads // n_tiles
        for h in range(per_tile):
            rot = rope(val[:, h * head_dim:(h + 1) * head_dim], cos_ref[...], sin_ref[...], even_lanes())
            q_ref[pl.ds(step * per_tile + h, n_rows, stride=heads), :] = rot

    @pl.when(step == n_tiles)
    def _():
        k_rot = rope(proj(wk_ref, bk_ref), cos_ref[...], sin_ref[...], even_lanes())
        kf_ref[...] = k_rot
        kb_ref[...] = k_rot.astype(jnp.bfloat16)
        v_new = proj(wv_ref, bv_ref)
        vf_ref[...] = v_new
        vb_ref[...] = v_new.astype(jnp.bfloat16)


def qkv(hidden, norm_w, w_q, b_q, w_k, b_k, w_v, b_v, positions, head_dim):
    n_rows, d_model = hidden.shape
    q_cols = w_q.shape[1]
    heads = q_cols // head_dim
    tile = 512
    n_tiles = q_cols // tile
    cos_t, sin_t = rope_tables(positions, head_dim)

    def whole(shape):
        return pl.BlockSpec(shape, lambda i: (0,) * len(shape))

    return pl.pallas_call(
        functools.partial(qkv_kernel, heads, n_tiles),
        grid=(n_tiles + 1,),
        in_specs=[
            whole((n_rows, d_model)), whole((1, d_model)),
            pl.BlockSpec((d_model, tile), lambda i: (0, jnp.minimum(i, n_tiles - 1))),
            pl.BlockSpec((1, tile), lambda i: (0, jnp.minimum(i, n_tiles - 1))),
            whole((d_model, head_dim)), whole((1, head_dim)), whole((d_model, head_dim)), whole((1, head_dim)),
            whole((n_rows, head_dim)), whole((n_rows, head_dim)),
        ],
        out_specs=[whole((n_rows * heads, head_dim))] + [whole((n_rows, head_dim))] * 4,
        out_shape=[
            jax.ShapeDtypeStruct((n_rows * heads, head_dim), jnp.float32),
            jax.ShapeDtypeStruct((n_rows, head_dim), jnp.float32),
            jax.ShapeDtypeStruct((n_rows, head_dim), jnp.float32),
            jax.ShapeDtypeStruct((n_rows, head_dim), jnp.bfloat16),
            jax.ShapeDtypeStruct((n_rows, head_dim), jnp.bfloat16),
        ],
        scratch_shapes=[pltpu.VMEM((n_rows, d_model), jnp.bfloat16)],
        compiler_params=pltpu.CompilerParams(vmem_limit_bytes=VMEM_LIMIT),
        name="qkv",
    )(hidden, norm_w[None], w_q, b_q[None], w_k, b_k[None], w_v, b_v[None], cos_t, sin_t)


def attn_kernel(seq_ref, q_ref, kf_ref, vf_ref, hid_hbm, k_hbm, v_hbm, wo_hbm, y_ref,
                o_buf, rd, rx, att, lhs, p_buf, p_recv, y_send, y_core, y_chip, y_fwd, wo, hid, kbuf, vbuf,
                k_sem, v_sem, wo_sem, hid_sem, rd_s, rd_r, rx_s, rx_r, at_s, at_r, p_s, p_r,
                yc_s, yc_r, yx_s, yx_r, yf_s, yf_r):
    n_rows, d_model = y_ref.shape
    s_dev, head_dim = kbuf.shape[2], kbuf.shape[3]
    heads = q_ref.shape[0] // n_rows
    half = wo.shape[0] * TN
    n_tiles = wo.shape[0]
    quarter = n_rows // (4 * NC)
    o_rows = quarter * heads
    chip_rows = n_rows // 2
    blk_per_q = quarter // BR
    n_blk = n_rows // BR
    coef = head_dim ** -0.5 * LOG2E

    dp, tp, sp = lax.axis_index("dp"), lax.axis_index("tp"), lax.axis_index("sp")
    chip, core = sp // 2, sp % 2
    to_core = (dp, tp, 2 * chip + (1 - core))
    to_chip = (dp, tp, 2 * (1 - chip) + core)
    to_tp = (dp, 1 - tp, sp)

    def remote(src, dst, s_sem, r_sem, dev):
        return pltpu.make_async_remote_copy(src_ref=src, dst_ref=dst, send_sem=s_sem, recv_sem=r_sem,
                                            device_id=dev, device_id_type=MESH)

    def quarter_row(n, qi):
        far = chip if qi >= 2 else 1 - chip
        owner_core = core if qi % 2 == 1 else 1 - core
        return far * chip_rows + n * 2 * quarter + owner_core * quarter

    def block_row(b):
        n = b // (4 * blk_per_q)
        r = b % (4 * blk_per_q)
        qi = r // blk_per_q
        w = r % blk_per_q
        own_chip = qi // 2
        own_core = qi % 2
        far = own_chip * chip + (1 - own_chip) * (1 - chip)
        o_core = own_core * core + (1 - own_core) * (1 - core)
        return pl.multiple_of(far * chip_rows + n * 2 * quarter + o_core * quarter + w * BR, BR)

    def kv_copies(b):
        slot = b % NB
        rows = pl.ds(block_row(b), BR)
        return (pltpu.make_async_copy(k_hbm.at[rows], kbuf.at[slot], k_sem.at[slot]),
                pltpu.make_async_copy(v_hbm.at[rows], vbuf.at[slot], v_sem.at[slot]))

    def start_kv(b):
        for c in kv_copies(b):
            c.start()

    def wo_copy(t):
        cols = pl.ds(pl.multiple_of(core * half + t * TN, 128), TN)
        return pltpu.make_async_copy(wo_hbm.at[:, cols], wo.at[t], wo_sem.at[t])

    hid_copy = pltpu.make_async_copy(
        hid_hbm.at[pl.ds(pl.multiple_of(chip * chip_rows, 128), chip_rows),
                   pl.ds(pl.multiple_of(core * half, 128), half)], hid, hid_sem)

    for b in range(NB):
        start_kv(b)

    barrier = pltpu.get_barrier_semaphore()
    for dev in (to_core, to_chip, to_tp):
        pl.semaphore_signal(barrier, inc=1, device_id=dev, device_id_type=MESH)
    pl.semaphore_wait(barrier, 3)

    lane = lax.broadcasted_iota(jnp.int32, (heads, head_dim), 1)
    pos = lax.broadcasted_iota(jnp.int32, (heads, s_dev), 1) + sp * s_dev
    is_first = sp == 0
    zeros_q = jnp.zeros((heads, head_dim), jnp.float32)

    def attend_quarter(n, qi):
        slot_o = n * 4 + qi
        base = (n * 4 + qi) * blk_per_q
        row_base = quarter_row(n, qi)

        def block(w, stats):
            m_all, l_all = stats
            b = base + w
            slot = b % NB
            row0 = pl.multiple_of(row_base + w * BR, BR)
            for c in kv_copies(b):
                c.wait()
            k_new = kf_ref[pl.ds(row0, BR), :]
            v_new = vf_ref[pl.ds(row0, BR), :]
            for pair in range(BR // 2):
                r = 2 * pair
                qs = [q_ref[pl.ds(pl.multiple_of((row0 + r + i) * heads, 8), heads), :] for i in range(2)]
                left = jnp.concatenate([qs[0], zeros_q], axis=0)
                right = jnp.concatenate([zeros_q, qs[1]], axis=0)
                q_pair = jnp.concatenate([left, right], axis=1).astype(jnp.bfloat16)
                k_pair = jnp.concatenate([kbuf[slot, r], kbuf[slot, r + 1]], axis=1)
                s_pair = lax.dot_general(q_pair, k_pair, (((1,), (1,)), ((), ())),
                                         preferred_element_type=jnp.float32)
                p_list, pn_list = [], []
                for i in range(2):
                    s = s_pair[i * heads:(i + 1) * heads]
                    s = jnp.where(pos < seq_ref[row0 + r + i], s, NEG)
                    s_new = jnp.sum(qs[i] * k_new[r + i:r + i + 1], axis=-1, keepdims=True)
                    s_new = jnp.where(is_first, s_new, NEG)
                    m = jnp.maximum(jnp.maximum(jnp.max(s, axis=-1, keepdims=True), s_new), NEG_FLOOR)
                    p = jnp.exp2((s - m) * coef)
                    p_new = jnp.exp2((s_new - m) * coef)
                    l = jnp.sum(p, axis=-1, keepdims=True) + p_new
                    here = lane == w * BR + r + i
                    m_all = jnp.where(here, m, m_all)
                    l_all = jnp.where(here, l, l_all)
                    p_list.append(p)
                    pn_list.append(p_new)
                p_pair = jnp.concatenate(p_list, axis=0).astype(jnp.bfloat16)
                v_pair = jnp.concatenate([vbuf[slot, r], vbuf[slot, r + 1]], axis=1)
                o_pair = jnp.dot(p_pair, v_pair, preferred_element_type=jnp.float32)
                for i in range(2):
                    o = o_pair[i * heads:(i + 1) * heads, i * head_dim:(i + 1) * head_dim]
                    o = o + pn_list[i] * v_new[r + i:r + i + 1]
                    o_buf[slot_o, pl.ds(pl.multiple_of((w * BR + r + i) * heads, 8), heads), :] = o

            @pl.when(b + NB < n_blk)
            def _():
                start_kv(b + NB)
            return m_all, l_all

        init = (jnp.zeros((heads, head_dim), jnp.float32), jnp.ones((heads, head_dim), jnp.float32))
        m_all, l_all = lax.fori_loop(0, blk_per_q, block, init)
        o_buf[slot_o, o_rows:o_rows + heads, :] = m_all
        o_buf[slot_o, o_rows + heads:o_rows + 2 * heads, :] = l_all

    def column(vals, j):
        return jnp.sum(jnp.where(lane == j, vals, 0.0), axis=-1, keepdims=True)

    def combine(slot_o, other, dst, final):
        m1 = o_buf[slot_o, o_rows:o_rows + heads, :]
        l1 = o_buf[slot_o, o_rows + heads:o_rows + 2 * heads, :]
        m2 = other[o_rows:o_rows + heads, :]
        l2 = other[o_rows + heads:o_rows + 2 * heads, :]
        m = jnp.maximum(m1, m2)
        f1 = jnp.exp2((m1 - m) * coef)
        f2 = jnp.exp2((m2 - m) * coef)
        l = l1 * f1 + l2 * f2
        if final:
            f1, f2 = f1 / l, f2 / l
        else:
            o_buf[slot_o, o_rows:o_rows + heads, :] = m
            o_buf[slot_o, o_rows + heads:o_rows + 2 * heads, :] = l

        def row(g, _):
            for u in range(4):
                j = g * 4 + u
                rows = pl.ds(pl.multiple_of(j * heads, 8), heads)
                o = o_buf[slot_o, rows, :] * column(f1, j) + other[rows, :] * column(f2, j)
                if final:
                    o = o.astype(jnp.bfloat16).astype(jnp.float32)
                dst[rows, :] = o
            return 0
        lax.fori_loop(0, quarter // 4, row, 0)

    def d2d(n, k):
        return remote(o_buf.at[n * 4 + 2 * k], rd.at[n * 2 + k], rd_s.at[n * 2 + k], rd_r.at[n * 2 + k], to_core)

    def xsend(n):
        return remote(o_buf.at[n * 4 + 1], rx.at[n], rx_s.at[n], rx_r.at[n], to_chip)

    def at_copy(n):
        return remote(att.at[n * 2 + core], att.at[n * 2 + core], at_s.at[n], at_r.at[n], to_core)

    def p_copy(i):
        return remote(p_buf.at[i], p_recv.at[i], p_s.at[i], p_r.at[i], to_tp)

    def yc_copy(i):
        return remote(y_send.at[i], y_core.at[i], yc_s.at[i], yc_r.at[i], to_core)

    def yx_copy(i):
        return remote(y_send.at[i], y_chip.at[i], yx_s.at[i], yx_r.at[i], to_chip)

    def yf_copy(i):
        return remote(y_chip.at[i], y_fwd.at[i], yf_s.at[i], yf_r.at[i], to_core)

    def finish(n):
        xsend(n).wait_recv()
        combine(n * 4 + 3, rx.at[n], att.at[n * 2 + core], True)
        at_copy(n).start()

    def project(n):
        at_copy(n).wait_recv()
        for h in range(heads):
            cols = [att[n * 2 + c, pl.ds(h, quarter, stride=heads), :] for c in range(2)]
            lhs[:, h * head_dim:(h + 1) * head_dim] = jnp.concatenate(cols, axis=0).astype(jnp.bfloat16)
        if n == 0:
            hid_copy.wait()

        def tile(t, _):
            if n == 0:
                wo_copy(t).wait()
            i = n * n_tiles + t
            p_buf[i] = jnp.dot(lhs[...], wo[t], preferred_element_type=jnp.float32)
            p_copy(i).start()
            return 0
        lax.fori_loop(0, n_tiles, tile, 0)

    def out_slice(i, on_chip, on_core):
        n, t = i // n_tiles, i % n_tiles
        rows = pl.ds(pl.multiple_of(on_chip * chip_rows + n * 2 * quarter, 2 * quarter), 2 * quarter)
        cols = pl.ds(pl.multiple_of(on_core * half + t * TN, TN), TN)
        return rows, cols

    def y_tile(i):
        n, t = i // n_tiles, i % n_tiles
        p_copy(i).wait_recv()
        res = hid[pl.ds(pl.multiple_of(n * 2 * quarter, 2 * quarter), 2 * quarter),
                  pl.ds(pl.multiple_of(t * TN, TN), TN)].astype(jnp.float32)
        y = (res + (p_buf[i] + p_recv[i])).astype(jnp.bfloat16)
        y_send[i] = y.astype(jnp.float32)
        rows, cols = out_slice(i, chip, core)
        y_ref[rows, cols] = y
        yx_copy(i).start()
        yc_copy(i).start()

    def y_from_chip(i):
        yx_copy(i).wait_recv()
        yf_copy(i).start()
        rows, cols = out_slice(i, 1 - chip, core)
        y_ref[rows, cols] = y_chip[i].astype(jnp.bfloat16)
        yc_copy(i).wait_recv()
        rows, cols = out_slice(i, chip, 1 - core)
        y_ref[rows, cols] = y_core[i].astype(jnp.bfloat16)

    def y_from_fwd(i):
        yf_copy(i).wait_recv()
        rows, cols = out_slice(i, 1 - chip, 1 - core)
        y_ref[rows, cols] = y_fwd[i].astype(jnp.bfloat16)

    wo_next = 0
    for n in range(NC):
        for qi in range(4):
            attend_quarter(n, qi)
            if qi == 0:
                d2d(n, 0).start()
            elif qi == 1:
                d2d(n, 0).wait_recv()
                combine(n * 4 + 1, rd.at[n * 2], o_buf.at[n * 4 + 1], False)
                xsend(n).start()
            elif qi == 2:
                d2d(n, 1).start()
            else:
                d2d(n, 1).wait_recv()
                combine(n * 4 + 3, rd.at[n * 2 + 1], o_buf.at[n * 4 + 3], False)
            if n == 0 and qi == 0:
                hid_copy.start()
            if wo_next < n_tiles:
                for _ in range(2):
                    wo_copy(wo_next).start()
                    wo_next += 1
            if n > 0 and qi == 1:
                finish(n - 1)
            if n > 0 and qi == 2:
                project(n - 1)
    finish(NC - 1)
    project(NC - 1)

    total = NC * n_tiles
    lag, lag2 = 2, 4

    def step(i, _):
        @pl.when(i < total)
        def _():
            y_tile(i)

        @pl.when(jnp.logical_and(i >= lag, i < total + lag))
        def _():
            y_from_chip(i - lag)

        @pl.when(i >= lag2)
        def _():
            y_from_fwd(i - lag2)
        return 0
    lax.fori_loop(0, total + lag2, step, 0)

    for n in range(NC):
        d2d(n, 0).wait_send()
        d2d(n, 1).wait_send()
        xsend(n).wait_send()
        at_copy(n).wait_send()

    def drain(i, _):
        p_copy(i).wait_send()
        yc_copy(i).wait_send()
        yx_copy(i).wait_send()
        yf_copy(i).wait_send()
        return 0
    lax.fori_loop(0, total, drain, 0)


def attention(seq_lens, q, kf, vf, hidden, k_cache, v_cache, w_o):
    n_rows, d_model = hidden.shape
    s_dev, head_dim = k_cache.shape[1], k_cache.shape[2]
    heads = q.shape[0] // n_rows
    half = d_model // 2
    n_tiles = half // TN
    quarter = n_rows // (4 * NC)
    msg = quarter * heads + 2 * heads
    total = NC * n_tiles
    vmem = pl.BlockSpec(memory_space=pltpu.VMEM)
    hbm = pl.BlockSpec(memory_space=pl.ANY)
    f32, bf16 = jnp.float32, jnp.bfloat16
    dma = pltpu.SemaphoreType.DMA
    tile_f32 = pltpu.VMEM((total, 2 * quarter, TN), f32)
    return pl.pallas_call(
        attn_kernel,
        out_shape=jax.ShapeDtypeStruct((n_rows, d_model), bf16),
        in_specs=[pl.BlockSpec(memory_space=pltpu.SMEM), vmem, vmem, vmem, hbm, hbm, hbm, hbm],
        out_specs=vmem,
        scratch_shapes=[
            pltpu.VMEM((NC * 4, msg, head_dim), f32),
            pltpu.VMEM((NC * 2, msg, head_dim), f32),
            pltpu.VMEM((NC, msg, head_dim), f32),
            pltpu.VMEM((NC * 2, quarter * heads, head_dim), f32),
            pltpu.VMEM((2 * quarter, heads * head_dim), bf16),
            tile_f32, tile_f32, tile_f32, tile_f32, tile_f32, tile_f32,
            pltpu.VMEM((n_tiles, heads * head_dim, TN), bf16),
            pltpu.VMEM((n_rows // 2, half), bf16),
            pltpu.VMEM((NB, BR, s_dev, head_dim), bf16),
            pltpu.VMEM((NB, BR, s_dev, head_dim), bf16),
            dma((NB,)), dma((NB,)), dma((n_tiles,)), dma,
            dma((NC * 2,)), dma((NC * 2,)), dma((NC,)), dma((NC,)), dma((NC,)), dma((NC,)),
            dma((total,)), dma((total,)), dma((total,)), dma((total,)), dma((total,)), dma((total,)),
            dma((total,)), dma((total,)),
        ],
        compiler_params=pltpu.CompilerParams(
            collective_id=0, has_side_effects=True, vmem_limit_bytes=VMEM_LIMIT),
        name="attend",
    )(seq_lens, q, kf, vf, hidden, k_cache, v_cache, w_o)


def solution(mesh):
    def device_step(hidden, norm_w, w_q, b_q, w_k, b_k, w_v, b_v, w_o, k_cache, v_cache, positions, seq_lens):
        n_rows = hidden.shape[0]
        s_dev, head_dim = k_cache.shape[1], k_cache.shape[3]
        q, kf, vf, kb, vb = qkv(hidden, norm_w, w_q, b_q, w_k, b_k, w_v, b_v, positions, head_dim)
        y_out = attention(seq_lens, q, kf, vf, hidden, k_cache.reshape(n_rows, s_dev, head_dim),
                          v_cache.reshape(n_rows, s_dev, head_dim), w_o)
        return y_out, kb.reshape(n_rows, 1, head_dim), vb.reshape(n_rows, 1, head_dim)

    col_spec = P(None, 'tp')
    vec_spec = P('tp')
    cache_spec = P('dp', 'sp', 'tp', None)
    group_spec = P('dp', 'tp', None)
    in_specs = (P('dp', None), P(None), col_spec, vec_spec, col_spec, vec_spec, col_spec, vec_spec,
                P('tp', None), cache_spec, cache_spec, P('dp'), P('dp'))
    out_specs = (P('dp', None), group_spec, group_spec)
    return jax.shard_map(device_step, mesh=mesh, in_specs=in_specs, out_specs=out_specs, check_vma=False)
```

time: 361 us -> 134 us (0.37)
  waiting for transfers between devices: 196 us -> 0 us
  Pallas kernels: 0 us -> 125 us
  matrix products: 86.1 us -> 0 us
  blocking collectives: 29.9 us -> 0 us
  other arithmetic: 27.4 us -> 1.92 us
  between operations: 14.4 us -> 0.64 us
    psum x2 -> x0, waiting for transfers between devices: 196 us -> none  [the longest x1 146 us: device_step(): lax.psum(jnp.dot(attn_rows, w_o, preferred_element_type=jnp.float32), 'tp')]
    pallas_call x0 -> x2, Pallas kernels: none -> 125 us  [the longest x1 101 us: attention(): pl.pallas_call(attn_kernel, out_shape=jax.ShapeDtypeStruct((n_rows, d_mod...]
    dot_general x7 -> x0, matrix products: 86.1 us -> none  [the longest x1 24.3 us: local_partials(): jnp.einsum('bgqd,bsgd->bgqs', q_grp, k_loc, preferred_element_type=jnp.fl...]
    pmax x1 -> x0, blocking collectives: 15 us -> none  [device_step(): m_all = lax.pmax(m_loc, 'sp')]
    psum x1 -> x0, blocking collectives: 14.8 us -> none  [device_step(): l_all, o_all = lax.psum((l_loc * factor, o_loc * factor[..., None]), 'sp')]
    reduce_sum x2 -> x0, other arithmetic: 13.2 us -> none  [the longest x1 10.6 us: local_partials(): l_loc = jnp.sum(p_cache, axis=-1) + p_new]
    convert_element_type x7 -> x1, other arithmetic: 11.1 us -> 0.68 us  [rope_tables(): angles = positions.astype(jnp.float32)[:, None] * freq]
  transfers between devices with their start and end apart: 2 -> 0, of which waited for: 2 -> 0; matrix products, arithmetic and copies ran while one was open for 0% -> 0% of each run, Pallas kernels for 0% -> 0%
where the time goes in v1:
time: 134 us
  Pallas kernels  125 us (93%)
  local copies, waits for them, and re-layouts  6.51 us (5%)
  other arithmetic  1.92 us (1%)
    pallas_call x1, Pallas kernels, attention(): pl.pallas_call(attn_kernel, out_shape=jax.ShapeDtypeStruct((n_rows, d_mod...  101 us
    pallas_call x1, Pallas kernels, qkv(): pl.pallas_call(functools.partial(qkv_kernel, heads, n_tiles), grid=(n_til...  24.2 us
    unnamed x1, local copies, waits for them, and re-layouts  3.88 us

profile of v1, /device:TPU:0, one launch (start us, length us, event | category | flops | bytes accessed | tf_op | source)
XLA Modules:
  0.0 133.9 jit_solution(7371145757345684488)
XLA Ops:
  0.6 0.7 convert_element_type.10
  1.3 1.3 broadcast_in_dim.28.bq_ref
  2.6 1.3 broadcast_in_dim.27.nw_ref
  4.0 1.2 fusion
  5.2 24.2 %qkv.1 = (f32[6144,128]{1,0:T(8,128)}, f32[256,128]{1,0:T(8,128)}, f32[256,128]{1,0:T(8,128)}, bf16[256,128]{1,0:T(8,128)(2,1)}, bf16[256,128]{1,0:T(8,128)(2,1)}) custom-call(bf16[256,6144]{1,0:T(8,128)(2,1)} %hid_hbm.1, bf16[1,6144]{1,0:T(2,128)(2,1)} %broadcast_in_dim.27.nw_ref, bf16[6144,3072]{1,0:T(8,128)(2,1)} %wq_ref.1, ...), custom_call_target="tpu_custom_call" | custom-call | tf_op jit(solution)/shard_map/qkv/pallas_call | solution.py:92
  29.4 100.6 %attend.1 = bf16[256,6144]{1,0:T(8,128)(2,1)} custom-call(s32[256]{0:T(256)} %seq_ref.1, f32[6144,128]{1,0:T(8,128)} %get-tuple-element.8.q_ref, f32[256,128]{1,0:T(8,128)} %get-tuple-element.9.kf_ref, f32[256,128]{1,0:T(8,128)} %get-tuple-element.10.vf_ref, bf16[256,6144]{1,0:T(8,128)(2,1)} %hid_hbm.1, bf16[256,512,128]{2,1,0:T(8,128)(2,1)} %bitcast.6, ...), custom_call_target="tpu_custom_call" | custom-call | tf_op jit(solution)/shard_map/attend/pallas_call | solution.py:424
  130.0 3.9 %copy.17 = bf16[256,6144]{1,0:T(8,128)(2,1)} copy(bf16[256,6144]{1,0:T(8,128)(2,1)} %attend.1) | data formatting | bytes 6291456
  (1 shorter events, 0.0 us)

commit v2 on v1

v2 whole, which is shorter than its diff:
```python
import functools

import jax
import jax.numpy as jnp
from jax import lax
from jax.experimental import pallas as pl
from jax.experimental.pallas import tpu as pltpu
from jax.sharding import PartitionSpec as P

RMS_EPS = 1.5625e-7
ROPE_BASE = 10000.0
LOG2E = 1.4426950408889634
NEG = -3e38
NEG_FLOOR = -1e38
MESH = pl.DeviceIdType.MESH
VMEM_LIMIT = 67_043_328

ATTN_VMEM = 59 * 2 ** 20

NC = 2
BR = 8
NBK, NBV = 4, 6
TN = 512
TS = 256


def rope_tables(positions, head_dim):
    rot_dim = head_dim // 2
    lane = jnp.arange(head_dim, dtype=jnp.int32)
    freq = ROPE_BASE ** (-2.0 * (lane // 2).astype(jnp.float32) / rot_dim)
    freq = jnp.where(lane < rot_dim, freq, 0.0)
    angles = positions.astype(jnp.float32)[:, None] * freq
    sign = jnp.where(lane % 2 == 0, -1.0, 1.0)
    return jnp.cos(angles), jnp.sin(angles) * sign


def rope(x, cos_t, sin_t, even):
    width = x.shape[-1]
    swapped = jnp.where(even, pltpu.roll(x, width - 1, 1), pltpu.roll(x, 1, 1))
    return (x * cos_t + swapped * sin_t).astype(jnp.bfloat16).astype(jnp.float32)


def qkv_kernel(heads, n_tiles, hid_ref, nw_ref, wq_ref, bq_ref, wk_ref, bk_ref, wv_ref, bv_ref, cos_ref, sin_ref,
               q_ref, kf_ref, vf_ref, kb_ref, vb_ref, normed):
    step = pl.program_id(0)
    n_rows, head_dim = cos_ref.shape

    @pl.when(step == 0)
    def _():
        def norm_rows(i, _):
            rows = pl.ds(pl.multiple_of(i * 32, 32), 32)
            x = hid_ref[rows, :].astype(jnp.float32)
            mean_sq = jnp.mean(x * x, axis=-1, keepdims=True)
            y = x * lax.rsqrt(mean_sq + RMS_EPS) * nw_ref[...].astype(jnp.float32)
            normed[rows, :] = y.astype(jnp.bfloat16)
            return 0
        lax.fori_loop(0, n_rows // 32, norm_rows, 0)

    def even_lanes():
        return lax.broadcasted_iota(jnp.int32, (n_rows, head_dim), 1) % 2 == 0

    def proj(w_ref, b_ref):
        acc = jnp.dot(normed[...], w_ref[...], preferred_element_type=jnp.float32)
        return (acc + b_ref[...].astype(jnp.float32)).astype(jnp.bfloat16).astype(jnp.float32)

    @pl.when(step < n_tiles)
    def _():
        val = proj(wq_ref, bq_ref)
        per_tile = heads // n_tiles
        for h in range(per_tile):
            rot = rope(val[:, h * head_dim:(h + 1) * head_dim], cos_ref[...], sin_ref[...], even_lanes())
            q_ref[pl.ds(step * per_tile + h, n_rows, stride=heads), :] = rot

    @pl.when(step == n_tiles)
    def _():
        k_rot = rope(proj(wk_ref, bk_ref), cos_ref[...], sin_ref[...], even_lanes())
        kf_ref[...] = k_rot
        kb_ref[...] = k_rot.astype(jnp.bfloat16)
        v_new = proj(wv_ref, bv_ref)
        vf_ref[...] = v_new
        vb_ref[...] = v_new.astype(jnp.bfloat16)


def qkv(hidden, norm_w, w_q, b_q, w_k, b_k, w_v, b_v, positions, head_dim):
    n_rows, d_model = hidden.shape
    q_cols = w_q.shape[1]
    heads = q_cols // head_dim
    tile = 512
    n_tiles = q_cols // tile
    cos_t, sin_t = rope_tables(positions, head_dim)

    def whole(shape):
        return pl.BlockSpec(shape, lambda i: (0,) * len(shape))

    return pl.pallas_call(
        functools.partial(qkv_kernel, heads, n_tiles),
        grid=(n_tiles + 1,),
        in_specs=[
            whole((n_rows, d_model)), whole((1, d_model)),
            pl.BlockSpec((d_model, tile), lambda i: (0, jnp.minimum(i, n_tiles - 1))),
            pl.BlockSpec((1, tile), lambda i: (0, jnp.minimum(i, n_tiles - 1))),
            whole((d_model, head_dim)), whole((1, head_dim)), whole((d_model, head_dim)), whole((1, head_dim)),
            whole((n_rows, head_dim)), whole((n_rows, head_dim)),
        ],
        out_specs=[whole((n_rows * heads, head_dim))] + [whole((n_rows, head_dim))] * 4,
        out_shape=[
            jax.ShapeDtypeStruct((n_rows * heads, head_dim), jnp.float32),
            jax.ShapeDtypeStruct((n_rows, head_dim), jnp.float32),
            jax.ShapeDtypeStruct((n_rows, head_dim), jnp.float32),
            jax.ShapeDtypeStruct((n_rows, head_dim), jnp.bfloat16),
            jax.ShapeDtypeStruct((n_rows, head_dim), jnp.bfloat16),
        ],
        scratch_shapes=[pltpu.VMEM((n_rows, d_model), jnp.bfloat16)],
        compiler_params=pltpu.CompilerParams(vmem_limit_bytes=VMEM_LIMIT),
        name="qkv",
    )(hidden, norm_w[None], w_q, b_q[None], w_k, b_k[None], w_v, b_v[None], cos_t, sin_t)


def attn_kernel(seq_ref, q_ref, kf_ref, vf_ref, hid_hbm, k_hbm, v_hbm, wo_hbm, y_ref,
                o_buf, rd, rx, att, lhs, s_sc, p_sc, new_sc, p_buf, p_recv, y_send, y_core, y_chip, y_fwd, wo, hid,
                kbuf, vbuf, k_sem, v_sem, wo_sem, hid_sem, rd_s, rd_r, rx_s, rx_r, at_s, at_r, p_s, p_r,
                yc_s, yc_r, yx_s, yx_r, yf_s, yf_r):
    n_rows, d_model = y_ref.shape
    s_dev, head_dim = kbuf.shape[2], kbuf.shape[3]
    heads = q_ref.shape[0] // n_rows
    n_tiles = wo.shape[0]
    half = n_tiles * TN
    quarter = n_rows // (4 * NC)
    o_rows = quarter * heads
    chip_rows = n_rows // 2
    bq = quarter // BR
    n_blk = n_rows // BR
    coef = head_dim ** -0.5 * LOG2E

    dp, tp, sp = lax.axis_index("dp"), lax.axis_index("tp"), lax.axis_index("sp")
    chip, core = sp // 2, sp % 2
    to_core = (dp, tp, 2 * chip + (1 - core))
    to_chip = (dp, tp, 2 * (1 - chip) + core)
    to_tp = (dp, 1 - tp, sp)

    def remote(src, dst, s_sem, r_sem, dev):
        return pltpu.make_async_remote_copy(src_ref=src, dst_ref=dst, send_sem=s_sem, recv_sem=r_sem,
                                            device_id=dev, device_id_type=MESH)

    def group_row(u):
        near = u // (2 * NC)
        own = u % 2
        n = (u % (2 * NC)) // 2
        on_chip = near * chip + (1 - near) * (1 - chip)
        on_core = own * core + (1 - own) * (1 - core)
        return on_chip * chip_rows + n * 2 * quarter + on_core * quarter

    def block_row(b):
        return pl.multiple_of(group_row(b // bq) + (b % bq) * BR, BR)

    def k_copy(b):
        return pltpu.make_async_copy(k_hbm.at[pl.ds(block_row(b), BR)], kbuf.at[b % NBK], k_sem.at[b % NBK])

    def v_copy(b):
        return pltpu.make_async_copy(v_hbm.at[pl.ds(block_row(b), BR)], vbuf.at[b % NBV], v_sem.at[b % NBV])

    def wo_copy(t):
        cols = pl.ds(pl.multiple_of(core * half + t * TN, 128), TN)
        return pltpu.make_async_copy(wo_hbm.at[:, cols], wo.at[t], wo_sem.at[t])

    hid_copy = pltpu.make_async_copy(
        hid_hbm.at[pl.ds(pl.multiple_of(chip * chip_rows, 128), chip_rows),
                   pl.ds(pl.multiple_of(core * half, 128), half)], hid, hid_sem)

    for b in range(NBV):
        if b < NBK:
            k_copy(b).start()
        v_copy(b).start()

    barrier = pltpu.get_barrier_semaphore()
    for dev in (to_core, to_chip, to_tp):
        pl.semaphore_signal(barrier, inc=1, device_id=dev, device_id_type=MESH)

    lane = lax.broadcasted_iota(jnp.int32, (heads, head_dim), 1)
    pos = lax.broadcasted_iota(jnp.int32, (heads, s_dev), 1) + sp * s_dev
    zeros_q = jnp.zeros((heads, head_dim), jnp.float32)

    def q_rows(row):
        return q_ref[pl.ds(pl.multiple_of(row * heads, 8), heads), :]

    def new_scores(n):
        row0 = chip * chip_rows + n * 2 * quarter + core * quarter

        def rows8(g, acc):
            base = pl.multiple_of(row0 + g * 8, 8)
            k_new = kf_ref[pl.ds(base, 8), :]
            for r in range(8):
                s_new = jnp.sum(q_rows(base + r) * k_new[r:r + 1], axis=-1, keepdims=True)
                acc = jnp.where(lane == g * 8 + r, s_new, acc)
            return acc
        new_sc[n] = lax.fori_loop(0, quarter // 8, rows8, zeros_q)

    for n in range(NC):
        new_scores(n)
    pl.semaphore_wait(barrier, 3)

    def column(vals, j):
        return jnp.sum(jnp.where(lane == j, vals, 0.0), axis=-1, keepdims=True)

    def d2d(k):
        return remote(o_buf.at[2 * k], rd.at[k], rd_s.at[k], rd_r.at[k], to_core)

    def xsend(n):
        return remote(o_buf.at[2 * n + 1], rx.at[n], rx_s.at[n], rx_r.at[n], to_chip)

    def at_copy(n):
        return remote(att.at[n * 2 + core], att.at[n * 2 + core], at_s.at[n], at_r.at[n], to_core)

    def merge_core(u):
        k = u // 2
        m1 = o_buf[u, o_rows:o_rows + heads, :]
        l1 = o_buf[u, o_rows + heads:o_rows + 2 * heads, :]
        m2 = rd[k, o_rows:o_rows + heads, :]
        l2 = rd[k, o_rows + heads:o_rows + 2 * heads, :]
        m = jnp.maximum(m1, m2)
        f1 = jnp.exp2((m1 - m) * coef)
        f2 = jnp.exp2((m2 - m) * coef)
        o_buf[u, o_rows:o_rows + heads, :] = m
        o_buf[u, o_rows + heads:o_rows + 2 * heads, :] = l1 * f1 + l2 * f2

        def rows8(g, _):
            for r in range(8):
                j = g * 8 + r
                rows = pl.ds(pl.multiple_of(j * heads, 8), heads)
                o_buf[u, rows, :] = o_buf[u, rows, :] * column(f1, j) + rd[k, rows, :] * column(f2, j)
            return 0
        lax.fori_loop(0, quarter // 8, rows8, 0)

    def finish(n):
        u = 2 * NC + 2 * n + 1
        row0 = chip * chip_rows + n * 2 * quarter + core * quarter
        m1 = o_buf[u, o_rows:o_rows + heads, :]
        l1 = o_buf[u, o_rows + heads:o_rows + 2 * heads, :]
        m2 = rx[n, o_rows:o_rows + heads, :]
        l2 = rx[n, o_rows + heads:o_rows + 2 * heads, :]
        m3 = new_sc[n]
        m = jnp.maximum(jnp.maximum(m1, m2), m3)
        f1 = jnp.exp2((m1 - m) * coef)
        f2 = jnp.exp2((m2 - m) * coef)
        f3 = jnp.exp2((m3 - m) * coef)
        l = l1 * f1 + l2 * f2 + f3
        f1, f2, f3 = f1 / l, f2 / l, f3 / l

        def rows8(g, _):
            v_new = vf_ref[pl.ds(pl.multiple_of(row0 + g * 8, 8), 8), :]
            for r in range(8):
                j = g * 8 + r
                rows = pl.ds(pl.multiple_of(j * heads, 8), heads)
                o = o_buf[u, rows, :] * column(f1, j) + rx[n, rows, :] * column(f2, j)
                o = o + column(f3, j) * v_new[r:r + 1]
                att[n * 2 + core, rows, :] = o.astype(jnp.bfloat16).astype(jnp.float32)
            return 0
        lax.fori_loop(0, quarter // 8, rows8, 0)

    def block(b, _):
        @pl.when(b < n_blk)
        def _():
            k_copy(b).wait()

        b1 = jnp.minimum(b, n_blk - 1)
        b2 = jnp.clip(b - 1, 0, n_blk - 1)
        b3 = jnp.clip(b - 2, 0, n_blk - 1)

        @pl.when(jnp.logical_or(b == 0, b >= 3))
        def _():
            v_copy(b3).wait()

        u3, vslot = b3 // bq, b3 % NBV
        for pair in range(BR // 2):
            r = 2 * pair
            v_pair = jnp.concatenate([vbuf[vslot, r], vbuf[vslot, r + 1]], axis=1)
            o_pair = jnp.dot(p_sc[pair], v_pair, preferred_element_type=jnp.float32)
            for i in range(2):
                o = o_pair[i * heads:(i + 1) * heads, i * head_dim:(i + 1) * head_dim]
                o_buf[u3, pl.ds(pl.multiple_of(((b3 % bq) * BR + r + i) * heads, 8), heads), :] = o
        u2, row2 = b2 // bq, block_row(b2)
        m_all = o_buf[u2, o_rows:o_rows + heads, :]
        l_all = o_buf[u2, o_rows + heads:o_rows + 2 * heads, :]
        for pair in range(BR // 2):
            p_list = []
            for i in range(2):
                r = 2 * pair + i
                s = s_sc[pair, i * heads:(i + 1) * heads, :]
                s = jnp.where(pos < seq_ref[row2 + r], s, NEG)
                m = jnp.maximum(jnp.max(s, axis=-1, keepdims=True), NEG_FLOOR)
                p = jnp.exp2((s - m) * coef)
                l = jnp.sum(p, axis=-1, keepdims=True)
                here = lane == (b2 % bq) * BR + r
                m_all = jnp.where(here, m, m_all)
                l_all = jnp.where(here, l, l_all)
                p_list.append(p)
            p_sc[pair] = jnp.concatenate(p_list, axis=0).astype(jnp.bfloat16)
        o_buf[u2, o_rows:o_rows + heads, :] = m_all
        o_buf[u2, o_rows + heads:o_rows + 2 * heads, :] = l_all
        row1, kslot = block_row(b1), b1 % NBK
        for pair in range(BR // 2):
            r = 2 * pair
            left = jnp.concatenate([q_rows(row1 + r), zeros_q], axis=0)
            right = jnp.concatenate([zeros_q, q_rows(row1 + r + 1)], axis=0)
            q_pair = jnp.concatenate([left, right], axis=1).astype(jnp.bfloat16)
            k_pair = jnp.concatenate([kbuf[kslot, r], kbuf[kslot, r + 1]], axis=1)
            s_sc[pair] = lax.dot_general(q_pair, k_pair, (((1,), (1,)), ((), ())),
                                         preferred_element_type=jnp.float32)

        @pl.when(b + NBK < n_blk)
        def _():
            k_copy(b + NBK).start()

        @pl.when(jnp.logical_and(b >= 2, b - 2 + NBV < n_blk))
        def _():
            v_copy(b - 2 + NBV).start()

        done = jnp.logical_and(b >= 2, (b - 2) % bq == bq - 1)
        u = b3 // bq

        @pl.when(jnp.logical_and(done, u % 2 == 0))
        def _():
            d2d(u // 2).start()

        @pl.when(jnp.logical_and(done, u % 2 == 1))
        def _():
            d2d(u // 2).wait_recv()
            merge_core(u)

            @pl.when(u < 2 * NC)
            def _():
                xsend(u // 2).start()
        return 0

    lax.fori_loop(0, n_blk + 2, block, 0)
    for t in range(n_tiles):
        wo_copy(t).start()
        if t == 0:
            hid_copy.start()

    def finish_step(n, _):
        xsend(n).wait_recv()
        finish(n)
        at_copy(n).start()
        return 0
    lax.fori_loop(0, NC, finish_step, 0)

    def p_copy(i):
        return remote(p_buf.at[i], p_recv.at[i], p_s.at[i], p_r.at[i], to_tp)

    def yc_copy(i):
        return remote(y_send.at[i], y_core.at[i], yc_s.at[i], yc_r.at[i], to_core)

    def yx_copy(i):
        return remote(y_send.at[i], y_chip.at[i], yx_s.at[i], yx_r.at[i], to_chip)

    def yf_copy(i):
        return remote(y_chip.at[i], y_fwd.at[i], yf_s.at[i], yf_r.at[i], to_core)

    for n in range(NC):
        at_copy(n).wait_recv()
        for h in range(heads):
            cols = [att[n * 2 + c, pl.ds(h, quarter, stride=heads), :] for c in range(2)]
            lhs[n * 2 * quarter:(n + 1) * 2 * quarter, h * head_dim:(h + 1) * head_dim] = (
                jnp.concatenate(cols, axis=0).astype(jnp.bfloat16))
    hid_copy.wait()
    per = TN // TS

    def project(t, _):
        wo_copy(t).wait()
        res = jnp.dot(lhs[...], wo[t], preferred_element_type=jnp.float32)
        for s in range(per):
            i = t * per + s
            p_buf[i] = res[:, s * TS:(s + 1) * TS]
            p_copy(i).start()
        return 0

    def out_cols(i, on_core):
        return pl.ds(pl.multiple_of(on_core * half + i * TS, TS), TS)

    def out_rows(on_chip):
        return pl.ds(pl.multiple_of(on_chip * chip_rows, chip_rows), chip_rows)

    def y_tile(i):
        p_copy(i).wait_recv()
        res = hid[:, pl.ds(pl.multiple_of(i * TS, TS), TS)].astype(jnp.float32)
        y = (res + (p_buf[i] + p_recv[i])).astype(jnp.bfloat16)
        y_send[i] = y.astype(jnp.float32)
        y_ref[out_rows(chip), out_cols(i, core)] = y
        yx_copy(i).start()
        yc_copy(i).start()

    def y_from_chip(i):
        yx_copy(i).wait_recv()
        yf_copy(i).start()
        y_ref[out_rows(1 - chip), out_cols(i, core)] = y_chip[i].astype(jnp.bfloat16)
        yc_copy(i).wait_recv()
        y_ref[out_rows(chip), out_cols(i, 1 - core)] = y_core[i].astype(jnp.bfloat16)

    def y_from_fwd(i):
        yf_copy(i).wait_recv()
        y_ref[out_rows(1 - chip), out_cols(i, 1 - core)] = y_fwd[i].astype(jnp.bfloat16)

    total = n_tiles * per
    lead = 2
    for t in range(lead):
        project(t, 0)
    lag, lag2 = 2, 3

    def step(i, _):
        @pl.when(jnp.logical_and(i % per == 0, i // per + lead < n_tiles))
        def _():
            project(i // per + lead, 0)

        @pl.when(i < total)
        def _():
            y_tile(i)

        @pl.when(jnp.logical_and(i >= lag, i < total + lag))
        def _():
            y_from_chip(i - lag)

        @pl.when(i >= lag2)
        def _():
            y_from_fwd(i - lag2)
        return 0
    lax.fori_loop(0, total + lag2, step, 0)

    for k in range(2 * NC):
        d2d(k).wait_send()
    for n in range(NC):
        xsend(n).wait_send()
        at_copy(n).wait_send()

    def drain(i, _):
        p_copy(i).wait_send()
        yc_copy(i).wait_send()
        yx_copy(i).wait_send()
        yf_copy(i).wait_send()
        return 0
    lax.fori_loop(0, total, drain, 0)


def attention(seq_lens, q, kf, vf, hidden, k_cache, v_cache, w_o):
    n_rows, d_model = hidden.shape
    s_dev, head_dim = k_cache.shape[1], k_cache.shape[2]
    heads = q.shape[0] // n_rows
    half = d_model // 2
    n_tiles = half // TN
    quarter = n_rows // (4 * NC)
    msg = quarter * heads + 2 * heads
    total = half // TS
    vmem = pl.BlockSpec(memory_space=pltpu.VMEM)
    hbm = pl.BlockSpec(memory_space=pl.ANY)
    f32, bf16 = jnp.float32, jnp.bfloat16
    dma = pltpu.SemaphoreType.DMA
    tile_f32 = pltpu.VMEM((total, n_rows // 2, TS), f32)
    return pl.pallas_call(
        attn_kernel,
        out_shape=jax.ShapeDtypeStruct((n_rows, d_model), bf16),
        in_specs=[pl.BlockSpec(memory_space=pltpu.SMEM), vmem, vmem, vmem, hbm, hbm, hbm, hbm],
        out_specs=vmem,
        scratch_shapes=[
            pltpu.VMEM((NC * 4, msg, head_dim), f32),
            pltpu.VMEM((NC * 2, msg, head_dim), f32),
            pltpu.VMEM((NC, msg, head_dim), f32),
            pltpu.VMEM((NC * 2, quarter * heads, head_dim), f32),
            pltpu.VMEM((n_rows // 2, heads * head_dim), bf16),
            pltpu.VMEM((BR // 2, 2 * heads, s_dev), f32),
            pltpu.VMEM((BR // 2, 2 * heads, s_dev), bf16),
            pltpu.VMEM((NC, heads, head_dim), f32),
            tile_f32, tile_f32, tile_f32, tile_f32, tile_f32, tile_f32,
            pltpu.VMEM((n_tiles, heads * head_dim, TN), bf16),
            pltpu.VMEM((n_rows // 2, half), bf16),
            pltpu.VMEM((NBK, BR, s_dev, head_dim), bf16),
            pltpu.VMEM((NBV, BR, s_dev, head_dim), bf16),
            dma((NBK,)), dma((NBV,)), dma((n_tiles,)), dma,
            dma((NC * 2,)), dma((NC * 2,)), dma((NC,)), dma((NC,)), dma((NC,)), dma((NC,)),
            dma((total,)), dma((total,)), dma((total,)), dma((total,)), dma((total,)), dma((total,)),
            dma((total,)), dma((total,)),
        ],
        compiler_params=pltpu.CompilerParams(
            collective_id=0, has_side_effects=True, vmem_limit_bytes=ATTN_VMEM),
        name="attend",
    )(seq_lens, q, kf, vf, hidden, k_cache, v_cache, w_o)


def solution(mesh):
    def device_step(hidden, norm_w, w_q, b_q, w_k, b_k, w_v, b_v, w_o, k_cache, v_cache, positions, seq_lens):
        n_rows = hidden.shape[0]
        s_dev, head_dim = k_cache.shape[1], k_cache.shape[3]
        q, kf, vf, kb, vb = qkv(hidden, norm_w, w_q, b_q, w_k, b_k, w_v, b_v, positions, head_dim)
        y_out = attention(seq_lens, q, kf, vf, hidden, k_cache.reshape(n_rows, s_dev, head_dim),
                          v_cache.reshape(n_rows, s_dev, head_dim), w_o)
        return y_out, kb.reshape(n_rows, 1, head_dim), vb.reshape(n_rows, 1, head_dim)

    col_spec = P(None, 'tp')
    vec_spec = P('tp')
    cache_spec = P('dp', 'sp', 'tp', None)
    group_spec = P('dp', 'tp', None)
    in_specs = (P('dp', None), P(None), col_spec, vec_spec, col_spec, vec_spec, col_spec, vec_spec,
                P('tp', None), cache_spec, cache_spec, P('dp'), P('dp'))
    out_specs = (P('dp', None), group_spec, group_spec)
    return jax.shard_map(device_step, mesh=mesh, in_specs=in_specs, out_specs=out_specs, check_vma=False)
```

time: 134 us -> 116 us (0.87)
  Pallas kernels: 125 us -> 106 us
    pallas_call x1, Pallas kernels: 101 us -> 82 us  [attention(): pl.pallas_call(attn_kernel, out_shape=jax.ShapeDtypeStruct((n_rows, d_mod...]
where the time goes in v2:
time: 116 us; the launch traced here: 115 us
  Pallas kernels  106 us (91%)
  local copies, waits for them, and re-layouts  6.51 us (6%)
  other arithmetic  1.92 us (2%)
    pallas_call x1, Pallas kernels, attention(): pl.pallas_call(attn_kernel, out_shape=jax.ShapeDtypeStruct((n_rows, d_mod...  82 us
    pallas_call x1, Pallas kernels, qkv(): pl.pallas_call(functools.partial(qkv_kernel, heads, n_tiles), grid=(n_til...  24.2 us
    unnamed x1, local copies, waits for them, and re-layouts  3.88 us

profile of v2, /device:TPU:0, one launch (start us, length us, event | category | flops | bytes accessed | tf_op | source)
XLA Modules:
  0.0 115.3 jit_solution(17442451053467386602)
XLA Ops:
  0.6 0.7 convert_element_type.10
  1.3 1.3 %broadcast_in_dim.28.bq_ref = bf16[1,3072]{1,0:T(2,128)(2,1)} reshape(bf16[3072]{0:T(1024)(128)(2,1)} %param.16) | data formatting | bytes 12288 | tf_op jit(solution)/shard_map/broadcast_in_dim | solution.py:116
  2.6 1.3 %broadcast_in_dim.27.nw_ref = bf16[1,6144]{1,0:T(2,128)(2,1)} reshape(bf16[6144]{0:T(1024)(128)(2,1)} %param.14) | data formatting | bytes 24576 | tf_op jit(solution)/shard_map/broadcast_in_dim | solution.py:116
  4.0 1.2 %fusion = (f32[256,128]{1,0:T(8,128)}, f32[256,128]{1,0:T(8,128)}) fusion(f32[128]{0:T(128)S(1)} %get-tuple-element.15, f32[128]{0:T(128)S(1)} %get-tuple-element.16, f32[256]{0:T(256)S(1)} %convert_element_type.10), kind=kLoop, calls=%fused_computation.2 | loop fusion | flops 65536 | bytes 264192 | tf_op jit(solution)/shard_map/mul | solution.py:34
  5.2 24.2 %qkv.1 = (f32[6144,128]{1,0:T(8,128)}, f32[256,128]{1,0:T(8,128)}, f32[256,128]{1,0:T(8,128)}, bf16[256,128]{1,0:T(8,128)(2,1)}, bf16[256,128]{1,0:T(8,128)(2,1)}) custom-call(bf16[256,6144]{1,0:T(8,128)(2,1)} %hid_hbm.1, bf16[1,6144]{1,0:T(2,128)(2,1)} %broadcast_in_dim.27.nw_ref, bf16[6144,3072]{1,0:T(8,128)(2,1)} %wq_ref.1, ...), custom_call_target="tpu_custom_call" | custom-call | tf_op jit(solution)/shard_map/qkv/pallas_call | solution.py:95
  29.4 82.0 %attend.1 = bf16[256,6144]{1,0:T(8,128)(2,1)} custom-call(s32[256]{0:T(256)} %seq_ref.1, f32[6144,128]{1,0:T(8,128)} %get-tuple-element.8.q_ref, f32[256,128]{1,0:T(8,128)} %get-tuple-element.9.kf_ref, f32[256,128]{1,0:T(8,128)} %get-tuple-element.10.vf_ref, bf16[256,6144]{1,0:T(8,128)(2,1)} %hid_hbm.1, bf16[256,512,128]{2,1,0:T(8,128)(2,1)} %bitcast.6, ...), custom_call_target="tpu_custom_call" | custom-call | tf_op jit(solution)/shard_map/attend/pallas_call | solution.py:458
  111.4 3.9 %copy.17 = bf16[256,6144]{1,0:T(8,128)(2,1)} copy(bf16[256,6144]{1,0:T(8,128)(2,1)} %attend.1) | data formatting | bytes 6291456
  (1 shorter events, 0.0 us)

commit v3 on v2

--- a/solution.py
+++ b/solution.py
@@ -15,7 +15,6 @@
 MESH = pl.DeviceIdType.MESH
 VMEM_LIMIT = 67_043_328
 
-ATTN_VMEM = 59 * 2 ** 20
 
 NC = 2
 BR = 8
@@ -40,84 +39,9 @@
     return (x * cos_t + swapped * sin_t).astype(jnp.bfloat16).astype(jnp.float32)
 
 
-def qkv_kernel(heads, n_tiles, hid_ref, nw_ref, wq_ref, bq_ref, wk_ref, bk_ref, wv_ref, bv_ref, cos_ref, sin_ref,
-               q_ref, kf_ref, vf_ref, kb_ref, vb_ref, normed):
-    step = pl.program_id(0)
-    n_rows, head_dim = cos_ref.shape
-
-    @pl.when(step == 0)
-    def _():
-        def norm_rows(i, _):
-            rows = pl.ds(pl.multiple_of(i * 32, 32), 32)
-            x = hid_ref[rows, :].astype(jnp.float32)
-            mean_sq = jnp.mean(x * x, axis=-1, keepdims=True)
-            y = x * lax.rsqrt(mean_sq + RMS_EPS) * nw_ref[...].astype(jnp.float32)
-            normed[rows, :] = y.astype(jnp.bfloat16)
-            return 0
-        lax.fori_loop(0, n_rows // 32, norm_rows, 0)
-
-    def even_lanes():
-        return lax.broadcasted_iota(jnp.int32, (n_rows, head_dim), 1) % 2 == 0
-
-    def proj(w_ref, b_ref):
-        acc = jnp.dot(normed[...], w_ref[...], preferred_element_type=jnp.float32)
-        return (acc + b_ref[...].astype(jnp.float32)).astype(jnp.bfloat16).astype(jnp.float32)
-
-    @pl.when(step < n_tiles)
-    def _():
-        val = proj(wq_ref, bq_ref)
-        per_tile = heads // n_tiles
-        for h in range(per_tile):
-            rot = rope(val[:, h * head_dim:(h + 1) * head_dim], cos_ref[...], sin_ref[...], even_lanes())
-            q_ref[pl.ds(step * per_tile + h, n_rows, stride=heads), :] = rot
-
-    @pl.when(step == n_tiles)
-    def _():
-        k_rot = rope(proj(wk_ref, bk_ref), cos_ref[...], sin_ref[...], even_lanes())
-        kf_ref[...] = k_rot
-        kb_ref[...] = k_rot.astype(jnp.bfloat16)
-        v_new = proj(wv_ref, bv_ref)
-        vf_ref[...] = v_new
-        vb_ref[...] = v_new.astype(jnp.bfloat16)
-
-
-def qkv(hidden, norm_w, w_q, b_q, w_k, b_k, w_v, b_v, positions, head_dim):
-    n_rows, d_model = hidden.shape
-    q_cols = w_q.shape[1]
-    heads = q_cols // head_dim
-    tile = 512
-    n_tiles = q_cols // tile
-    cos_t, sin_t = rope_tables(positions, head_dim)
-
-    def whole(shape):
-        return pl.BlockSpec(shape, lambda i: (0,) * len(shape))
-
-    return pl.pallas_call(
-        functools.partial(qkv_kernel, heads, n_tiles),
-        grid=(n_tiles + 1,),
-        in_specs=[
-            whole((n_rows, d_model)), whole((1, d_model)),
-            pl.BlockSpec((d_model, tile), lambda i: (0, jnp.minimum(i, n_tiles - 1))),
-            pl.BlockSpec((1, tile), lambda i: (0, jnp.minimum(i, n_tiles - 1))),
-            whole((d_model, head_dim)), whole((1, head_dim)), whole((d_model, head_dim)), whole((1, head_dim)),
-            whole((n_rows, head_dim)), whole((n_rows, head_dim)),
-        ],
-        out_specs=[whole((n_rows * heads, head_dim))] + [whole((n_rows, head_dim))] * 4,
-        out_shape=[
-            jax.ShapeDtypeStruct((n_rows * heads, head_dim), jnp.float32),
-            jax.ShapeDtypeStruct((n_rows, head_dim), jnp.float32),
-            jax.ShapeDtypeStruct((n_rows, head_dim), jnp.float32),
-            jax.ShapeDtypeStruct((n_rows, head_dim), jnp.bfloat16),
-            jax.ShapeDtypeStruct((n_rows, head_dim), jnp.bfloat16),
-        ],
-        scratch_shapes=[pltpu.VMEM((n_rows, d_model), jnp.bfloat16)],
-        compiler_params=pltpu.CompilerParams(vmem_limit_bytes=VMEM_LIMIT),
-        name="qkv",
-    )(hidden, norm_w[None], w_q, b_q[None], w_k, b_k[None], w_v, b_v[None], cos_t, sin_t)
-
-
-def attn_kernel(seq_ref, q_ref, kf_ref, vf_ref, hid_hbm, k_hbm, v_hbm, wo_hbm, y_ref,
-                o_buf, rd, rx, att, lhs, s_sc, p_sc, new_sc, p_buf, p_recv, y_send, y_core, y_chip, y_fwd, wo, hid,
+def attn_kernel(seq_ref, cos_ref, sin_ref, nw_ref, bq_ref, bk_ref, bv_ref, hid_hbm, wq_hbm, wk_hbm, wv_hbm,
+                k_hbm, v_hbm, wo_hbm, y_ref, kb_ref, vb_ref,
+                q_ref, q_send, q_recv, wkv, bqf, kf_ref, vf_ref, in_sem, wkv_sem, q_s, q_r, o_buf, rd, rx, att, lhs, s_sc, p_sc, new_sc, p_buf, p_recv, y_send, y_core, y_chip, y_fwd, wo, hid,
                 kbuf, vbuf, k_sem, v_sem, wo_sem, hid_sem, rd_s, rd_r, rx_s, rx_r, at_s, at_r, p_s, p_r,
                 yc_s, yc_r, yx_s, yx_r, yf_s, yf_r):
     n_rows, d_model = y_ref.shape
@@ -167,14 +91,92 @@
         hid_hbm.at[pl.ds(pl.multiple_of(chip * chip_rows, 128), chip_rows),
                    pl.ds(pl.multiple_of(core * half, 128), half)], hid, hid_sem)
 
-    for b in range(NBV):
-        if b < NBK:
-            k_copy(b).start()
-        v_copy(b).start()
+    n_q = q_send.shape[0]
+    tile_heads = TN // head_dim
+    k_half = wo.shape[1]
+    in_copy = pltpu.make_async_copy(hid_hbm, y_ref, in_sem)
+    wk_copy = pltpu.make_async_copy(wk_hbm, wkv.at[:, :head_dim], wkv_sem.at[0])
+    wv_copy = pltpu.make_async_copy(wv_hbm, wkv.at[:, head_dim:], wkv_sem.at[1])
+
+    def wq_copy(i):
+        cols = pl.ds(pl.multiple_of((core * n_q + i // 2) * TN, TN), TN)
+        return pltpu.make_async_copy(wq_hbm.at[pl.ds((i % 2) * k_half, k_half), cols], wo.at[i], wo_sem.at[i])
+
+    in_copy.start()
+    wk_copy.start()
+    wv_copy.start()
+    for i in range(2 * n_q):
+        wq_copy(i).start()
 
     barrier = pltpu.get_barrier_semaphore()
     for dev in (to_core, to_chip, to_tp):
         pl.semaphore_signal(barrier, inc=1, device_id=dev, device_id_type=MESH)
+
+    bqf[...] = bq_ref[...].astype(jnp.float32)
+    in_copy.wait()
+
+    def norm_rows(i, _):
+        rows = pl.ds(pl.multiple_of(i * 32, 32), 32)
+        sq = jnp.zeros((32, 128), jnp.float32)
+        for c in range(d_model // 128):
+            x = y_ref[rows, c * 128:(c + 1) * 128].astype(jnp.float32)
+            sq = sq + x * x
+        inv = lax.rsqrt(jnp.sum(sq, axis=-1, keepdims=True) / d_model + RMS_EPS)
+        for c in range(d_model // 128):
+            x = y_ref[rows, c * 128:(c + 1) * 128].astype(jnp.float32)
+            x = x * inv * nw_ref[c:c + 1, :].astype(jnp.float32)
+            y_ref[rows, c * 128:(c + 1) * 128] = x.astype(jnp.bfloat16)
+        return 0
+    lax.fori_loop(0, n_rows // 32, norm_rows, 0)
+    pl.semaphore_wait(barrier, 3)
+
+    even = lax.broadcasted_iota(jnp.int32, (n_rows, head_dim), 1) % 2 == 0
+
+    def round_f32(x):
+        return x.astype(jnp.bfloat16).astype(jnp.float32)
+
+    wk_copy.wait()
+    wv_copy.wait()
+    kv = jnp.dot(y_ref[...], wkv[...], preferred_element_type=jnp.float32)
+    k_rot = rope(round_f32(kv[:, :head_dim] + bk_ref[...].astype(jnp.float32)), cos_ref[...], sin_ref[...], even)
+    kf_ref[...] = k_rot
+    kb_ref[...] = k_rot.astype(jnp.bfloat16)
+    v_val = round_f32(kv[:, head_dim:] + bv_ref[...].astype(jnp.float32))
+    vf_ref[...] = v_val
+    vb_ref[...] = v_val.astype(jnp.bfloat16)
+
+    def q_copy(t):
+        return remote(q_send.at[t], q_recv.at[t], q_s.at[t], q_r.at[t], to_core)
+
+    def q_tile(t, _):
+        wq_copy(2 * t).wait()
+        wq_copy(2 * t + 1).wait()
+
+        @pl.when(t == n_q - 1)
+        def _():
+            for b in range(NBV):
+                if b < NBK:
+                    k_copy(b).start()
+                v_copy(b).start()
+        acc = jnp.dot(y_ref[:, :k_half], wo[2 * t], preferred_element_type=jnp.float32)
+        acc = acc + jnp.dot(y_ref[:, k_half:], wo[2 * t + 1], preferred_element_type=jnp.float32)
+        for h in range(tile_heads):
+            head = core * (heads // 2) + t * tile_heads + h
+            val = round_f32(acc[:, h * head_dim:(h + 1) * head_dim] + bqf[pl.ds(head, 1), :])
+            val = rope(val, cos_ref[...], sin_ref[...], even)
+            q_ref[pl.ds(head, n_rows, stride=heads), :] = val
+            q_send[t, pl.ds(h, n_rows, stride=tile_heads), :] = val
+        q_copy(t).start()
+        return 0
+    lax.fori_loop(0, n_q, q_tile, 0)
+
+    def q_take(t, _):
+        q_copy(t).wait_recv()
+        for h in range(tile_heads):
+            head = (1 - core) * (heads // 2) + t * tile_heads + h
+            q_ref[pl.ds(head, n_rows, stride=heads), :] = q_recv[t, pl.ds(h, n_rows, stride=tile_heads), :]
+        return 0
+    lax.fori_loop(0, n_q, q_take, 0)
 
     lane = lax.broadcasted_iota(jnp.int32, (heads, head_dim), 1)
     pos = lax.broadcasted_iota(jnp.int32, (heads, s_dev), 1) + sp * s_dev
@@ -197,10 +199,9 @@
 
     for n in range(NC):
         new_scores(n)
-    pl.semaphore_wait(barrier, 3)
 
     def column(vals, j):
-        return jnp.sum(jnp.where(lane == j, vals, 0.0), axis=-1, keepdims=True)
+        return jnp.broadcast_to(vals[:, j:j + 1], (heads, head_dim))
 
     def d2d(k):
         return remote(o_buf.at[2 * k], rd.at[k], rd_s.at[k], rd_r.at[k], to_core)
@@ -223,13 +224,9 @@
         o_buf[u, o_rows:o_rows + heads, :] = m
         o_buf[u, o_rows + heads:o_rows + 2 * heads, :] = l1 * f1 + l2 * f2
 
-        def rows8(g, _):
-            for r in range(8):
-                j = g * 8 + r
-                rows = pl.ds(pl.multiple_of(j * heads, 8), heads)
-                o_buf[u, rows, :] = o_buf[u, rows, :] * column(f1, j) + rd[k, rows, :] * column(f2, j)
-            return 0
-        lax.fori_loop(0, quarter // 8, rows8, 0)
+        for j in range(quarter):
+            rows = pl.ds(j * heads, heads)
+            o_buf[u, rows, :] = o_buf[u, rows, :] * column(f1, j) + rd[k, rows, :] * column(f2, j)
 
     def finish(n):
         u = 2 * NC + 2 * n + 1
@@ -246,16 +243,13 @@
         l = l1 * f1 + l2 * f2 + f3
         f1, f2, f3 = f1 / l, f2 / l, f3 / l
 
-        def rows8(g, _):
-            v_new = vf_ref[pl.ds(pl.multiple_of(row0 + g * 8, 8), 8), :]
-            for r in range(8):
-                j = g * 8 + r
-                rows = pl.ds(pl.multiple_of(j * heads, 8), heads)
-                o = o_buf[u, rows, :] * column(f1, j) + rx[n, rows, :] * column(f2, j)
-                o = o + column(f3, j) * v_new[r:r + 1]
-                att[n * 2 + core, rows, :] = o.astype(jnp.bfloat16).astype(jnp.float32)
-            return 0
-        lax.fori_loop(0, quarter // 8, rows8, 0)
+        for j in range(quarter):
+            if j % 8 == 0:
+                v_new = vf_ref[pl.ds(pl.multiple_of(row0 + j, 8), 8), :]
+            rows = pl.ds(j * heads, heads)
+            o = o_buf[u, rows, :] * column(f1, j) + rx[n, rows, :] * column(f2, j)
+            o = o + column(f3, j) * v_new[j % 8:j % 8 + 1]
+            att[n * 2 + core, rows, :] = round_f32(o)
 
     def block(b, _):
         @pl.when(b < n_blk)
@@ -426,6 +420,8 @@
         return 0
     lax.fori_loop(0, total + lag2, step, 0)
 
+    for t in range(n_q):
+        q_copy(t).wait_send()
     for k in range(2 * NC):
         d2d(k).wait_send()
     for n in range(NC):
@@ -441,12 +437,13 @@
     lax.fori_loop(0, total, drain, 0)
 
 
-def attention(seq_lens, q, kf, vf, hidden, k_cache, v_cache, w_o):
+def attention(seq_lens, cos_t, sin_t, norm_w, b_q, b_k, b_v, hidden, w_q, w_k, w_v, k_cache, v_cache, w_o):
     n_rows, d_model = hidden.shape
     s_dev, head_dim = k_cache.shape[1], k_cache.shape[2]
-    heads = q.shape[0] // n_rows
+    heads = w_q.shape[1] // head_dim
     half = d_model // 2
     n_tiles = half // TN
+    n_q = w_q.shape[1] // (2 * TN)
     quarter = n_rows // (4 * NC)
     msg = quarter * heads + 2 * heads
     total = half // TS
@@ -457,10 +454,17 @@
     tile_f32 = pltpu.VMEM((total, n_rows // 2, TS), f32)
     return pl.pallas_call(
         attn_kernel,
-        out_shape=jax.ShapeDtypeStruct((n_rows, d_model), bf16),
-        in_specs=[pl.BlockSpec(memory_space=pltpu.SMEM), vmem, vmem, vmem, hbm, hbm, hbm, hbm],
-        out_specs=vmem,
+        out_shape=[jax.ShapeDtypeStruct((n_rows, d_model), bf16)] + [jax.ShapeDtypeStruct((n_rows, head_dim), bf16)] * 2,
+        in_specs=[pl.BlockSpec(memory_space=pltpu.SMEM)] + [vmem] * 6 + [hbm] * 7,
+        out_specs=[vmem] * 3,
         scratch_shapes=[
+            pltpu.VMEM((n_rows * heads, head_dim), f32),
+            pltpu.VMEM((n_q, n_rows * TN // head_dim, head_dim), f32),
+            pltpu.VMEM((n_q, n_rows * TN // head_dim, head_dim), f32),
+            pltpu.VMEM((d_model, 2 * head_dim), bf16),
+            pltpu.VMEM((heads, head_dim), f32),
+            pltpu.VMEM((n_rows, head_dim), f32), pltpu.VMEM((n_rows, head_dim), f32),
+            dma, dma((2,)), dma((n_q,)), dma((n_q,)),
             pltpu.VMEM((NC * 4, msg, head_dim), f32),
             pltpu.VMEM((NC * 2, msg, head_dim), f32),
             pltpu.VMEM((NC, msg, head_dim), f32),
@@ -480,18 +484,49 @@
             dma((total,)), dma((total,)),
         ],
         compiler_params=pltpu.CompilerParams(
-            collective_id=0, has_side_effects=True, vmem_limit_bytes=ATTN_VMEM),
+            collective_id=0, has_side_effects=True, vmem_limit_bytes=VMEM_LIMIT),
         name="attend",
-    )(seq_lens, q, kf, vf, hidden, k_cache, v_cache, w_o)
+    )(seq_lens, cos_t, sin_t, norm_w.reshape(-1, 128), b_q.reshape(heads, head_dim), b_k[None], b_v[None], hidden,
+      w_q, w_k, w_v, k_cache, v_cache, w_o)
+
+
+def copy_kernel(parts, y_in, k_in, v_in, y_out, k_out, v_out, buf, kv_buf, in_sem, out_sem):
+    rows = y_in.shape[0] // parts
+    pairs = [(y_in.at[pl.ds(p * rows, rows)], buf.at[p], y_out.at[pl.ds(p * rows, rows)]) for p in range(parts)]
+    pairs += [(k_in, kv_buf.at[0], k_out), (v_in, kv_buf.at[1], v_out)]
+    loads = [pltpu.make_async_copy(a, m, in_sem.at[i]) for i, (a, m, _) in enumerate(pairs)]
+    stores = [pltpu.make_async_copy(m, z, out_sem.at[i]) for i, (_, m, z) in enumerate(pairs)]
+    for c in loads:
+        c.start()
+    for c, d in zip(loads, stores):
+        c.wait()
+        d.start()
+    for d in stores:
+        d.wait()
+
+
+def copy_out(y, k, v):
+    parts = 8
+    hbm = pl.BlockSpec(memory_space=pl.ANY)
+    dma = pltpu.SemaphoreType.DMA
+    return pl.pallas_call(
+        functools.partial(copy_kernel, parts),
+        out_shape=[jax.ShapeDtypeStruct(a.shape, a.dtype) for a in (y, k, v)],
+        in_specs=[hbm] * 3, out_specs=[hbm] * 3,
+        scratch_shapes=[pltpu.VMEM((parts, y.shape[0] // parts, y.shape[1]), y.dtype),
+                        pltpu.VMEM((2,) + k.shape, k.dtype), dma((parts + 2,)), dma((parts + 2,))],
+        name="copy_out",
+    )(y, k, v)
 
 
 def solution(mesh):
     def device_step(hidden, norm_w, w_q, b_q, w_k, b_k, w_v, b_v, w_o, k_cache, v_cache, positions, seq_lens):
         n_rows = hidden.shape[0]
         s_dev, head_dim = k_cache.shape[1], k_cache.shape[3]
-        q, kf, vf, kb, vb = qkv(hidden, norm_w, w_q, b_q, w_k, b_k, w_v, b_v, positions, head_dim)
-        y_out = attention(seq_lens, q, kf, vf, hidden, k_cache.reshape(n_rows, s_dev, head_dim),
-                          v_cache.reshape(n_rows, s_dev, head_dim), w_o)
+        cos_t, sin_t = rope_tables(positions, head_dim)
+        outs = attention(seq_lens, cos_t, sin_t, norm_w, b_q, b_k, b_v, hidden, w_q, w_k, w_v,
+                         k_cache.reshape(n_rows, s_dev, head_dim), v_cache.reshape(n_rows, s_dev, head_dim), w_o)
+        y_out, kb, vb = copy_out(*outs)
         return y_out, kb.reshape(n_rows, 1, head_dim), vb.reshape(n_rows, 1, head_dim)
 
     col_spec = P(None, 'tp')

time: 116 us -> 102 us (0.88)
  Pallas kernels: 106 us -> 99.4 us
  local copies, waits for them, and re-layouts: 6.51 us -> 0 us
    pallas_call x2, Pallas kernels: 106 us -> 99.4 us  [the longest x1 96.6 us: attention(): pl.pallas_call(attn_kernel, out_shape=[jax.ShapeDtypeStruct((n_rows, d_mo...]
    unnamed x1 -> x0, local copies, waits for them, and re-layouts: 3.88 us -> none
    broadcast_in_dim x2 -> x0, local copies, waits for them, and re-layouts: 2.63 us -> none  [the longest x1 1.33 us: qkv(): norm_w[None]]
where the time goes in v3:
time: 102 us
  Pallas kernels  99.4 us (97%)
  other arithmetic  1.94 us (2%)
    pallas_call x1, Pallas kernels, attention(): pl.pallas_call(attn_kernel, out_shape=[jax.ShapeDtypeStruct((n_rows, d_mo...  96.6 us
    pallas_call x1, Pallas kernels, copy_out(): pl.pallas_call(functools.partial(copy_kernel, parts), out_shape=[jax.Shap...  2.86 us

profile of v3, /device:TPU:0, one launch (start us, length us, event | category | flops | bytes accessed | tf_op | source)
XLA Modules:
  0.0 102.0 jit_solution(17903922350359146761)
XLA Ops:
  0.6 0.7 convert_element_type.10
  1.3 1.2 %fusion = (f32[256,128]{1,0:T(8,128)}, f32[256,128]{1,0:T(8,128)}) fusion(f32[128]{0:T(128)S(1)} %get-tuple-element.17, f32[128]{0:T(128)S(1)} %get-tuple-element.18, f32[256]{0:T(256)S(1)} %convert_element_type.10), kind=kLoop, calls=%fused_computation.2 | loop fusion | flops 65536 | bytes 264192 | tf_op jit(solution)/shard_map/mul | solution.py:33
  2.6 96.6 %attend.1 = (bf16[256,6144]{1,0:T(8,128)(2,1)}, bf16[256,128]{1,0:T(8,128)(2,1)}, bf16[256,128]{1,0:T(8,128)(2,1)}) custom-call(s32[256]{0:T(256)} %seq_ref.1, f32[256,128]{1,0:T(8,128)} %get-tuple-element.16.cos_ref, f32[256,128]{1,0:T(8,128)} %get-tuple-element.15.sin_ref, bf16[48,128]{1,0:T(8,128)(2,1)} %bitcast.10, bf16[24,128]{1,0:T(8,128)(2,1)} %bitcast.11, ...), custom_call_target="tpu_custom_call" | custom-call | tf_op jit(solution)/shard_map/attend/pallas_call | solution.py:455
  99.1 2.9 %copy_out.1 = (bf16[256,6144]{1,0:T(8,128)(2,1)}, bf16[256,128]{1,0:T(8,128)(2,1)}, bf16[256,128]{1,0:T(8,128)(2,1)}) custom-call(bf16[256,6144]{1,0:T(8,128)(2,1)} %get-tuple-element.9.y_in, bf16[256,128]{1,0:T(8,128)(2,1)} %get-tuple-element.10.k_in, bf16[256,128]{1,0:T(8,128)(2,1)} %get-tuple-element.11.v_in), custom_call_target="tpu_custom_call" | custom-call | tf_op jit(solution)/shard_map/copy_out/pallas_call | solution.py:512
  (1 shorter events, 0.0 us)

commit v4 on v3

--- a/solution.py
+++ b/solution.py
@@ -16,6 +16,7 @@
 VMEM_LIMIT = 67_043_328
 
 
+NORM_ROWS = 32
 NC = 2
 BR = 8
 NBK, NBV = 4, 6
@@ -94,7 +95,11 @@
     n_q = q_send.shape[0]
     tile_heads = TN // head_dim
     k_half = wo.shape[1]
-    in_copy = pltpu.make_async_copy(hid_hbm, y_ref, in_sem)
+
+    def in_copy(i):
+        rows = pl.ds(pl.multiple_of(i * NORM_ROWS, NORM_ROWS), NORM_ROWS)
+        return pltpu.make_async_copy(hid_hbm.at[rows], y_ref.at[rows], in_sem.at[i])
+
     wk_copy = pltpu.make_async_copy(wk_hbm, wkv.at[:, :head_dim], wkv_sem.at[0])
     wv_copy = pltpu.make_async_copy(wv_hbm, wkv.at[:, head_dim:], wkv_sem.at[1])
 
@@ -102,22 +107,29 @@
         cols = pl.ds(pl.multiple_of((core * n_q + i // 2) * TN, TN), TN)
         return pltpu.make_async_copy(wq_hbm.at[pl.ds((i % 2) * k_half, k_half), cols], wo.at[i], wo_sem.at[i])
 
-    in_copy.start()
-    wk_copy.start()
-    wv_copy.start()
-    for i in range(2 * n_q):
-        wq_copy(i).start()
+    n_norm = n_rows // NORM_ROWS
+    for i in range(n_norm):
+        in_copy(i).start()
 
     barrier = pltpu.get_barrier_semaphore()
     for dev in (to_core, to_chip, to_tp):
         pl.semaphore_signal(barrier, inc=1, device_id=dev, device_id_type=MESH)
 
     bqf[...] = bq_ref[...].astype(jnp.float32)
-    in_copy.wait()
 
     def norm_rows(i, _):
-        rows = pl.ds(pl.multiple_of(i * 32, 32), 32)
-        sq = jnp.zeros((32, 128), jnp.float32)
+        rows = pl.ds(pl.multiple_of(i * NORM_ROWS, NORM_ROWS), NORM_ROWS)
+        in_copy(i).wait()
+
+        @pl.when(i < 2 * n_q)
+        def _():
+            wq_copy(i).start()
+
+        @pl.when(i == n_norm - 1)
+        def _():
+            wk_copy.start()
+            wv_copy.start()
+        sq = jnp.zeros((NORM_ROWS, 128), jnp.float32)
         for c in range(d_model // 128):
             x = y_ref[rows, c * 128:(c + 1) * 128].astype(jnp.float32)
             sq = sq + x * x
@@ -127,23 +139,13 @@
             x = x * inv * nw_ref[c:c + 1, :].astype(jnp.float32)
             y_ref[rows, c * 128:(c + 1) * 128] = x.astype(jnp.bfloat16)
         return 0
-    lax.fori_loop(0, n_rows // 32, norm_rows, 0)
+    lax.fori_loop(0, n_norm, norm_rows, 0)
     pl.semaphore_wait(barrier, 3)
 
     even = lax.broadcasted_iota(jnp.int32, (n_rows, head_dim), 1) % 2 == 0
 
     def round_f32(x):
         return x.astype(jnp.bfloat16).astype(jnp.float32)
-
-    wk_copy.wait()
-    wv_copy.wait()
-    kv = jnp.dot(y_ref[...], wkv[...], preferred_element_type=jnp.float32)
-    k_rot = rope(round_f32(kv[:, :head_dim] + bk_ref[...].astype(jnp.float32)), cos_ref[...], sin_ref[...], even)
-    kf_ref[...] = k_rot
-    kb_ref[...] = k_rot.astype(jnp.bfloat16)
-    v_val = round_f32(kv[:, head_dim:] + bv_ref[...].astype(jnp.float32))
-    vf_ref[...] = v_val
-    vb_ref[...] = v_val.astype(jnp.bfloat16)
 
     def q_copy(t):
         return remote(q_send.at[t], q_recv.at[t], q_s.at[t], q_r.at[t], to_core)
@@ -169,6 +171,16 @@
         q_copy(t).start()
         return 0
     lax.fori_loop(0, n_q, q_tile, 0)
+
+    wk_copy.wait()
+    wv_copy.wait()
+    kv = jnp.dot(y_ref[...], wkv[...], preferred_element_type=jnp.float32)
+    k_rot = rope(round_f32(kv[:, :head_dim] + bk_ref[...].astype(jnp.float32)), cos_ref[...], sin_ref[...], even)
+    kf_ref[...] = k_rot
+    kb_ref[...] = k_rot.astype(jnp.bfloat16)
+    v_val = round_f32(kv[:, head_dim:] + bv_ref[...].astype(jnp.float32))
+    vf_ref[...] = v_val
+    vb_ref[...] = v_val.astype(jnp.bfloat16)
 
     def q_take(t, _):
         q_copy(t).wait_recv()
@@ -464,7 +476,7 @@
             pltpu.VMEM((d_model, 2 * head_dim), bf16),
             pltpu.VMEM((heads, head_dim), f32),
             pltpu.VMEM((n_rows, head_dim), f32), pltpu.VMEM((n_rows, head_dim), f32),
-            dma, dma((2,)), dma((n_q,)), dma((n_q,)),
+            dma((n_rows // NORM_ROWS,)), dma((2,)), dma((n_q,)), dma((n_q,)),
             pltpu.VMEM((NC * 4, msg, head_dim), f32),
             pltpu.VMEM((NC * 2, msg, head_dim), f32),
             pltpu.VMEM((NC, msg, head_dim), f32),

time: 102 us -> 97 us (0.951)
  Pallas kernels: 99.4 us -> 94.3 us
    pallas_call x1, Pallas kernels: 96.6 us -> 91.4 us  [attention(): pl.pallas_call(attn_kernel, out_shape=[jax.ShapeDtypeStruct((n_rows, d_mo...]
where the time goes in v4:
time: 97 us; the launch traced here: 96.8 us
  Pallas kernels  94.3 us (97%)
  other arithmetic  1.94 us (2%)
    pallas_call x1, Pallas kernels, attention(): pl.pallas_call(attn_kernel, out_shape=[jax.ShapeDtypeStruct((n_rows, d_mo...  91.4 us
    pallas_call x1, Pallas kernels, copy_out(): pl.pallas_call(functools.partial(copy_kernel, parts), out_shape=[jax.Shap...  2.86 us

profile of v4, /device:TPU:0, one launch (start us, length us, event | category | flops | bytes accessed | tf_op | source)
XLA Modules:
  0.0 96.8 jit_solution(17184456753730904522)
XLA Ops:
  0.6 0.7 convert_element_type.10
  1.3 1.2 %fusion = (f32[256,128]{1,0:T(8,128)}, f32[256,128]{1,0:T(8,128)}) fusion(f32[128]{0:T(128)S(1)} %get-tuple-element.17, f32[128]{0:T(128)S(1)} %get-tuple-element.18, f32[256]{0:T(256)S(1)} %convert_element_type.10), kind=kLoop, calls=%fused_computation.2 | loop fusion | flops 65536 | bytes 264192 | tf_op jit(solution)/shard_map/mul | solution.py:34
  2.6 91.4 %attend.1 = (bf16[256,6144]{1,0:T(8,128)(2,1)}, bf16[256,128]{1,0:T(8,128)(2,1)}, bf16[256,128]{1,0:T(8,128)(2,1)}) custom-call(s32[256]{0:T(256)} %seq_ref.1, f32[256,128]{1,0:T(8,128)} %get-tuple-element.16.cos_ref, f32[256,128]{1,0:T(8,128)} %get-tuple-element.15.sin_ref, bf16[48,128]{1,0:T(8,128)(2,1)} %bitcast.10, bf16[24,128]{1,0:T(8,128)(2,1)} %bitcast.11, ...), custom_call_target="tpu_custom_call" | custom-call | tf_op jit(solution)/shard_map/attend/pallas_call | solution.py:467
  94.0 2.9 %copy_out.1 = (bf16[256,6144]{1,0:T(8,128)(2,1)}, bf16[256,128]{1,0:T(8,128)(2,1)}, bf16[256,128]{1,0:T(8,128)(2,1)}) custom-call(bf16[256,6144]{1,0:T(8,128)(2,1)} %get-tuple-element.9.y_in, bf16[256,128]{1,0:T(8,128)(2,1)} %get-tuple-element.10.k_in, bf16[256,128]{1,0:T(8,128)(2,1)} %get-tuple-element.11.v_in), custom_call_target="tpu_custom_call" | custom-call | tf_op jit(solution)/shard_map/copy_out/pallas_call | solution.py:524
  (1 shorter events, 0.0 us)

commit v5 on v4

--- a/solution.py
+++ b/solution.py
@@ -263,7 +263,7 @@
             o = o + column(f3, j) * v_new[j % 8:j % 8 + 1]
             att[n * 2 + core, rows, :] = round_f32(o)
 
-    def block(b, _):
+    def block(b, new, old):
         @pl.when(b < n_blk)
         def _():
             k_copy(b).wait()
@@ -276,14 +276,6 @@
         def _():
             v_copy(b3).wait()
 
-        u3, vslot = b3 // bq, b3 % NBV
-        for pair in range(BR // 2):
-            r = 2 * pair
-            v_pair = jnp.concatenate([vbuf[vslot, r], vbuf[vslot, r + 1]], axis=1)
-            o_pair = jnp.dot(p_sc[pair], v_pair, preferred_element_type=jnp.float32)
-            for i in range(2):
-                o = o_pair[i * heads:(i + 1) * heads, i * head_dim:(i + 1) * head_dim]
-                o_buf[u3, pl.ds(pl.multiple_of(((b3 % bq) * BR + r + i) * heads, 8), heads), :] = o
         u2, row2 = b2 // bq, block_row(b2)
         m_all = o_buf[u2, o_rows:o_rows + heads, :]
         l_all = o_buf[u2, o_rows + heads:o_rows + 2 * heads, :]
@@ -291,7 +283,7 @@
             p_list = []
             for i in range(2):
                 r = 2 * pair + i
-                s = s_sc[pair, i * heads:(i + 1) * heads, :]
+                s = s_sc[old, pair, i * heads:(i + 1) * heads, :]
                 s = jnp.where(pos < seq_ref[row2 + r], s, NEG)
                 m = jnp.maximum(jnp.max(s, axis=-1, keepdims=True), NEG_FLOOR)
                 p = jnp.exp2((s - m) * coef)
@@ -300,7 +292,7 @@
                 m_all = jnp.where(here, m, m_all)
                 l_all = jnp.where(here, l, l_all)
                 p_list.append(p)
-            p_sc[pair] = jnp.concatenate(p_list, axis=0).astype(jnp.bfloat16)
+            p_sc[new, pair] = jnp.concatenate(p_list, axis=0).astype(jnp.bfloat16)
         o_buf[u2, o_rows:o_rows + heads, :] = m_all
         o_buf[u2, o_rows + heads:o_rows + 2 * heads, :] = l_all
         row1, kslot = block_row(b1), b1 % NBK
@@ -310,8 +302,16 @@
             right = jnp.concatenate([zeros_q, q_rows(row1 + r + 1)], axis=0)
             q_pair = jnp.concatenate([left, right], axis=1).astype(jnp.bfloat16)
             k_pair = jnp.concatenate([kbuf[kslot, r], kbuf[kslot, r + 1]], axis=1)
-            s_sc[pair] = lax.dot_general(q_pair, k_pair, (((1,), (1,)), ((), ())),
+            s_sc[new, pair] = lax.dot_general(q_pair, k_pair, (((1,), (1,)), ((), ())),
                                          preferred_element_type=jnp.float32)
+        u3, vslot = b3 // bq, b3 % NBV
+        for pair in range(BR // 2):
+            r = 2 * pair
+            v_pair = jnp.concatenate([vbuf[vslot, r], vbuf[vslot, r + 1]], axis=1)
+            o_pair = jnp.dot(p_sc[old, pair], v_pair, preferred_element_type=jnp.float32)
+            for i in range(2):
+                o = o_pair[i * heads:(i + 1) * heads, i * head_dim:(i + 1) * head_dim]
+                o_buf[u3, pl.ds(pl.multiple_of(((b3 % bq) * BR + r + i) * heads, 8), heads), :] = o
 
         @pl.when(b + NBK < n_blk)
         def _():
@@ -336,9 +336,13 @@
             @pl.when(u < 2 * NC)
             def _():
                 xsend(u // 2).start()
-        return 0
-
-    lax.fori_loop(0, n_blk + 2, block, 0)
+
+    def two_blocks(g, _):
+        block(2 * g, 0, 1)
+        block(2 * g + 1, 1, 0)
+        return 0
+
+    lax.fori_loop(0, (n_blk + 2) // 2, two_blocks, 0)
     for t in range(n_tiles):
         wo_copy(t).start()
         if t == 0:
@@ -482,8 +486,8 @@
             pltpu.VMEM((NC, msg, head_dim), f32),
             pltpu.VMEM((NC * 2, quarter * heads, head_dim), f32),
             pltpu.VMEM((n_rows // 2, heads * head_dim), bf16),
-            pltpu.VMEM((BR // 2, 2 * heads, s_dev), f32),
-            pltpu.VMEM((BR // 2, 2 * heads, s_dev), bf16),
+            pltpu.VMEM((2, BR // 2, 2 * heads, s_dev), f32),
+            pltpu.VMEM((2, BR // 2, 2 * heads, s_dev), bf16),
             pltpu.VMEM((NC, heads, head_dim), f32),
             tile_f32, tile_f32, tile_f32, tile_f32, tile_f32, tile_f32,
             pltpu.VMEM((n_tiles, heads * head_dim, TN), bf16),

time: 97 us -> 97.1 us (level)
  no operation moved by 1% of the time
where the time goes in v5:
time: 97.1 us; the launch traced here: 97 us
  Pallas kernels  94.4 us (97%)
  other arithmetic  1.94 us (2%)
    pallas_call x1, Pallas kernels, attention(): pl.pallas_call(attn_kernel, out_shape=[jax.ShapeDtypeStruct((n_rows, d_mo...  91.6 us
    pallas_call x1, Pallas kernels, copy_out(): pl.pallas_call(functools.partial(copy_kernel, parts), out_shape=[jax.Shap...  2.86 us

profile of v5, /device:TPU:0, one launch (start us, length us, event | category | flops | bytes accessed | tf_op | source)
XLA Modules:
  0.0 97.0 jit_solution(5266210466669828513)
XLA Ops:
  0.6 0.7 convert_element_type.10
  1.3 1.2 %fusion = (f32[256,128]{1,0:T(8,128)}, f32[256,128]{1,0:T(8,128)}) fusion(f32[128]{0:T(128)S(1)} %get-tuple-element.17, f32[128]{0:T(128)S(1)} %get-tuple-element.18, f32[256]{0:T(256)S(1)} %convert_element_type.10), kind=kLoop, calls=%fused_computation.2 | loop fusion | flops 65536 | bytes 264192 | tf_op jit(solution)/shard_map/mul | solution.py:34
  2.6 91.6 %attend.1 = (bf16[256,6144]{1,0:T(8,128)(2,1)}, bf16[256,128]{1,0:T(8,128)(2,1)}, bf16[256,128]{1,0:T(8,128)(2,1)}) custom-call(s32[256]{0:T(256)} %seq_ref.1, f32[256,128]{1,0:T(8,128)} %get-tuple-element.16.cos_ref, f32[256,128]{1,0:T(8,128)} %get-tuple-element.15.sin_ref, bf16[48,128]{1,0:T(8,128)(2,1)} %bitcast.10, bf16[24,128]{1,0:T(8,128)(2,1)} %bitcast.11, ...), custom_call_target="tpu_custom_call" | custom-call | tf_op jit(solution)/shard_map/attend/pallas_call | solution.py:471
  94.1 2.9 %copy_out.1 = (bf16[256,6144]{1,0:T(8,128)(2,1)}, bf16[256,128]{1,0:T(8,128)(2,1)}, bf16[256,128]{1,0:T(8,128)(2,1)}) custom-call(bf16[256,6144]{1,0:T(8,128)(2,1)} %get-tuple-element.9.y_in, bf16[256,128]{1,0:T(8,128)(2,1)} %get-tuple-element.10.k_in, bf16[256,128]{1,0:T(8,128)(2,1)} %get-tuple-element.11.v_in), custom_call_target="tpu_custom_call" | custom-call | tf_op jit(solution)/shard_map/copy_out/pallas_call | solution.py:528
  (1 shorter events, 0.0 us)

commit v6 on v5

--- a/solution.py
+++ b/solution.py
@@ -17,11 +17,13 @@
 
 
 NORM_ROWS = 32
-NC = 2
+NC = 4
+NH = 2
 BR = 8
 NBK, NBV = 4, 6
 TN = 512
-TS = 256
+G_FINISH, G_PROJECT = 12, 13
+WO_FROM = 14
 
 
 def rope_tables(positions, head_dim):
@@ -67,13 +69,24 @@
         return pltpu.make_async_remote_copy(src_ref=src, dst_ref=dst, send_sem=s_sem, recv_sem=r_sem,
                                             device_id=dev, device_id_type=MESH)
 
+    per_part = NC // NH
+    part_rows = chip_rows // NH
+
+    def group_piece(u):
+        return (u // (4 * per_part)) * per_part + (u % (2 * per_part)) // 2
+
+    def group_far(u):
+        return u % (4 * per_part) < 2 * per_part
+
     def group_row(u):
-        near = u // (2 * NC)
+        near = (u % (4 * per_part)) // (2 * per_part)
         own = u % 2
-        n = (u % (2 * NC)) // 2
         on_chip = near * chip + (1 - near) * (1 - chip)
         on_core = own * core + (1 - own) * (1 - core)
-        return on_chip * chip_rows + n * 2 * quarter + on_core * quarter
+        return on_chip * chip_rows + group_piece(u) * 2 * quarter + on_core * quarter
+
+    def kept_group(n, near):
+        return (n // per_part) * 4 * per_part + near * 2 * per_part + 2 * (n % per_part) + 1
 
     def block_row(b):
         return pl.multiple_of(group_row(b // bq) + (b % bq) * BR, BR)
@@ -219,7 +232,7 @@
         return remote(o_buf.at[2 * k], rd.at[k], rd_s.at[k], rd_r.at[k], to_core)
 
     def xsend(n):
-        return remote(o_buf.at[2 * n + 1], rx.at[n], rx_s.at[n], rx_r.at[n], to_chip)
+        return remote(o_buf.at[kept_group(n, 0)], rx.at[n], rx_s.at[n], rx_r.at[n], to_chip)
 
     def at_copy(n):
         return remote(att.at[n * 2 + core], att.at[n * 2 + core], at_s.at[n], at_r.at[n], to_core)
@@ -241,7 +254,7 @@
             o_buf[u, rows, :] = o_buf[u, rows, :] * column(f1, j) + rd[k, rows, :] * column(f2, j)
 
     def finish(n):
-        u = 2 * NC + 2 * n + 1
+        u = kept_group(n, 1)
         row0 = chip * chip_rows + n * 2 * quarter + core * quarter
         m1 = o_buf[u, o_rows:o_rows + heads, :]
         l1 = o_buf[u, o_rows + heads:o_rows + 2 * heads, :]
@@ -321,6 +334,16 @@
         def _():
             v_copy(b - 2 + NBV).start()
 
+        w = b - WO_FROM
+
+        @pl.when(jnp.logical_and(w >= 0, jnp.logical_and(w % 2 == 0, w < 2 * n_tiles)))
+        def _():
+            wo_copy(w // 2).start()
+
+        @pl.when(w == 2 * n_tiles)
+        def _():
+            hid_copy.start()
+
         done = jnp.logical_and(b >= 2, (b - 2) % bq == bq - 1)
         u = b3 // bq
 
@@ -333,28 +356,15 @@
             d2d(u // 2).wait_recv()
             merge_core(u)
 
-            @pl.when(u < 2 * NC)
+            @pl.when(group_far(u))
             def _():
-                xsend(u // 2).start()
+                xsend(group_piece(u)).start()
 
     def two_blocks(g, _):
         block(2 * g, 0, 1)
         block(2 * g + 1, 1, 0)
         return 0
 
-    lax.fori_loop(0, (n_blk + 2) // 2, two_blocks, 0)
-    for t in range(n_tiles):
-        wo_copy(t).start()
-        if t == 0:
-            hid_copy.start()
-
-    def finish_step(n, _):
-        xsend(n).wait_recv()
-        finish(n)
-        at_copy(n).start()
-        return 0
-    lax.fori_loop(0, NC, finish_step, 0)
-
     def p_copy(i):
         return remote(p_buf.at[i], p_recv.at[i], p_s.at[i], p_r.at[i], to_tp)
 
@@ -367,74 +377,96 @@
     def yf_copy(i):
         return remote(y_chip.at[i], y_fwd.at[i], yf_s.at[i], yf_r.at[i], to_core)
 
-    for n in range(NC):
-        at_copy(n).wait_recv()
-        for h in range(heads):
-            cols = [att[n * 2 + c, pl.ds(h, quarter, stride=heads), :] for c in range(2)]
-            lhs[n * 2 * quarter:(n + 1) * 2 * quarter, h * head_dim:(h + 1) * head_dim] = (
-                jnp.concatenate(cols, axis=0).astype(jnp.bfloat16))
-    hid_copy.wait()
-    per = TN // TS
-
-    def project(t, _):
-        wo_copy(t).wait()
-        res = jnp.dot(lhs[...], wo[t], preferred_element_type=jnp.float32)
-        for s in range(per):
-            i = t * per + s
-            p_buf[i] = res[:, s * TS:(s + 1) * TS]
+    def finish_part(h):
+        for k in range(per_part):
+            n = h * per_part + k
+            xsend(n).wait_recv()
+            finish(n)
+            at_copy(n).start()
+
+    def project_part(h):
+        for k in range(per_part):
+            n = h * per_part + k
+            at_copy(n).wait_recv()
+            for hd in range(heads):
+                cols = [att[n * 2 + c, pl.ds(hd, quarter, stride=heads), :] for c in range(2)]
+                lhs[k * 2 * quarter:(k + 1) * 2 * quarter, hd * head_dim:(hd + 1) * head_dim] = (
+                    jnp.concatenate(cols, axis=0).astype(jnp.bfloat16))
+
+        def tile(t, _):
+            if h == 0:
+                wo_copy(t).wait()
+            i = h * n_tiles + t
+            p_buf[i] = jnp.dot(lhs[...], wo[t], preferred_element_type=jnp.float32)
             p_copy(i).start()
-        return 0
+            return 0
+        lax.fori_loop(0, n_tiles, tile, 0)
 
     def out_cols(i, on_core):
-        return pl.ds(pl.multiple_of(on_core * half + i * TS, TS), TS)
-
-    def out_rows(on_chip):
-        return pl.ds(pl.multiple_of(on_chip * chip_rows, chip_rows), chip_rows)
+        return pl.ds(pl.multiple_of(on_core * half + (i % n_tiles) * TN, TN), TN)
+
+    def out_rows(i, on_chip):
+        return pl.ds(pl.multiple_of(on_chip * chip_rows + (i // n_tiles) * part_rows, part_rows), part_rows)
 
     def y_tile(i):
         p_copy(i).wait_recv()
-        res = hid[:, pl.ds(pl.multiple_of(i * TS, TS), TS)].astype(jnp.float32)
+        res = hid[pl.ds(pl.multiple_of((i // n_tiles) * part_rows, part_rows), part_rows),
+                  pl.ds(pl.multiple_of((i % n_tiles) * TN, TN), TN)].astype(jnp.float32)
         y = (res + (p_buf[i] + p_recv[i])).astype(jnp.bfloat16)
         y_send[i] = y.astype(jnp.float32)
-        y_ref[out_rows(chip), out_cols(i, core)] = y
+        y_ref[out_rows(i, chip), out_cols(i, core)] = y
         yx_copy(i).start()
         yc_copy(i).start()
 
     def y_from_chip(i):
         yx_copy(i).wait_recv()
         yf_copy(i).start()
-        y_ref[out_rows(1 - chip), out_cols(i, core)] = y_chip[i].astype(jnp.bfloat16)
+        y_ref[out_rows(i, 1 - chip), out_cols(i, core)] = y_chip[i].astype(jnp.bfloat16)
         yc_copy(i).wait_recv()
-        y_ref[out_rows(chip), out_cols(i, 1 - core)] = y_core[i].astype(jnp.bfloat16)
+        y_ref[out_rows(i, chip), out_cols(i, 1 - core)] = y_core[i].astype(jnp.bfloat16)
 
     def y_from_fwd(i):
         yf_copy(i).wait_recv()
-        y_ref[out_rows(1 - chip), out_cols(i, 1 - core)] = y_fwd[i].astype(jnp.bfloat16)
-
-    total = n_tiles * per
-    lead = 2
-    for t in range(lead):
-        project(t, 0)
-    lag, lag2 = 2, 3
-
-    def step(i, _):
-        @pl.when(jnp.logical_and(i % per == 0, i // per + lead < n_tiles))
-        def _():
-            project(i // per + lead, 0)
-
-        @pl.when(i < total)
-        def _():
-            y_tile(i)
-
-        @pl.when(jnp.logical_and(i >= lag, i < total + lag))
-        def _():
-            y_from_chip(i - lag)
-
-        @pl.when(i >= lag2)
-        def _():
-            y_from_fwd(i - lag2)
-        return 0
-    lax.fori_loop(0, total + lag2, step, 0)
+        y_ref[out_rows(i, 1 - chip), out_cols(i, 1 - core)] = y_fwd[i].astype(jnp.bfloat16)
+
+    total = NH * n_tiles
+    last = (n_blk + 2) // 2
+    lax.fori_loop(0, G_FINISH, two_blocks, 0)
+    finish_part(0)
+    lax.fori_loop(G_FINISH, G_PROJECT, two_blocks, 0)
+    project_part(0)
+
+    def two_blocks_and_tile(g, _):
+        two_blocks(g, 0)
+
+        @pl.when(g == last - 3)
+        def _():
+            hid_copy.wait()
+
+        @pl.when(jnp.logical_or(g == last - 3, g == last - 1))
+        def _():
+            y_tile((g - (last - 3)) // 2)
+        return 0
+    lax.fori_loop(G_PROJECT, last, two_blocks_and_tile, 0)
+    finish_part(1)
+    y_tile(2)
+    project_part(1)
+    early = 3
+
+    def step(s, _):
+        @pl.when(s + early < total)
+        def _():
+            y_tile(s + early)
+
+        @pl.when(s < total)
+        def _():
+            y_from_chip(s)
+
+        @pl.when(s >= 1)
+        def _():
+            y_from_fwd(s - 1)
+        return 0
+    lax.fori_loop(0, total + 1, step, 0)
 
     for t in range(n_q):
         q_copy(t).wait_send()
@@ -462,12 +494,12 @@
     n_q = w_q.shape[1] // (2 * TN)
     quarter = n_rows // (4 * NC)
     msg = quarter * heads + 2 * heads
-    total = half // TS
+    total = NH * n_tiles
     vmem = pl.BlockSpec(memory_space=pltpu.VMEM)
     hbm = pl.BlockSpec(memory_space=pl.ANY)
     f32, bf16 = jnp.float32, jnp.bfloat16
     dma = pltpu.SemaphoreType.DMA
-    tile_f32 = pltpu.VMEM((total, n_rows // 2, TS), f32)
+    tile_f32 = pltpu.VMEM((total, n_rows // (2 * NH), TN), f32)
     return pl.pallas_call(
         attn_kernel,
         out_shape=[jax.ShapeDtypeStruct((n_rows, d_model), bf16)] + [jax.ShapeDtypeStruct((n_rows, head_dim), bf16)] * 2,
@@ -485,7 +517,7 @@
             pltpu.VMEM((NC * 2, msg, head_dim), f32),
             pltpu.VMEM((NC, msg, head_dim), f32),
             pltpu.VMEM((NC * 2, quarter * heads, head_dim), f32),
-            pltpu.VMEM((n_rows // 2, heads * head_dim), bf16),
+            pltpu.VMEM((n_rows // (2 * NH), heads * head_dim), bf16),
             pltpu.VMEM((2, BR // 2, 2 * heads, s_dev), f32),
             pltpu.VMEM((2, BR // 2, 2 * heads, s_dev), bf16),
             pltpu.VMEM((NC, heads, head_dim), f32),

time: 97.1 us -> 88.9 us (0.916)
  Pallas kernels: 94.4 us -> 86.2 us
    pallas_call x1, Pallas kernels: 91.6 us -> 83.4 us  [attention(): pl.pallas_call(attn_kernel, out_shape=[jax.ShapeDtypeStruct((n_rows, d_mo...]
where the time goes in v6:
time: 88.9 us; the launch traced here: 88.8 us
  Pallas kernels  86.2 us (97%)
  other arithmetic  1.94 us (2%)
    pallas_call x1, Pallas kernels, attention(): pl.pallas_call(attn_kernel, out_shape=[jax.ShapeDtypeStruct((n_rows, d_mo...  83.4 us
    pallas_call x1, Pallas kernels, copy_out(): pl.pallas_call(functools.partial(copy_kernel, parts), out_shape=[jax.Shap...  2.86 us

profile of v6, /device:TPU:0, one launch (start us, length us, event | category | flops | bytes accessed | tf_op | source)
XLA Modules:
  0.0 88.8 jit_solution(8322074471143637723)
XLA Ops:
  0.6 0.7 convert_element_type.10
  1.3 1.2 %fusion = (f32[256,128]{1,0:T(8,128)}, f32[256,128]{1,0:T(8,128)}) fusion(f32[128]{0:T(128)S(1)} %get-tuple-element.17, f32[128]{0:T(128)S(1)} %get-tuple-element.18, f32[256]{0:T(256)S(1)} %convert_element_type.10), kind=kLoop, calls=%fused_computation.2 | loop fusion | flops 65536 | bytes 264192 | tf_op jit(solution)/shard_map/mul | solution.py:36
  2.6 83.4 %attend.1 = (bf16[256,6144]{1,0:T(8,128)(2,1)}, bf16[256,128]{1,0:T(8,128)(2,1)}, bf16[256,128]{1,0:T(8,128)(2,1)}) custom-call(s32[256]{0:T(256)} %seq_ref.1, f32[256,128]{1,0:T(8,128)} %get-tuple-element.16.cos_ref, f32[256,128]{1,0:T(8,128)} %get-tuple-element.15.sin_ref, bf16[48,128]{1,0:T(8,128)(2,1)} %bitcast.10, bf16[24,128]{1,0:T(8,128)(2,1)} %bitcast.11, ...), custom_call_target="tpu_custom_call" | custom-call | tf_op jit(solution)/shard_map/attend/pallas_call | solution.py:503
  85.9 2.9 %copy_out.1 = (bf16[256,6144]{1,0:T(8,128)(2,1)}, bf16[256,128]{1,0:T(8,128)(2,1)}, bf16[256,128]{1,0:T(8,128)(2,1)}) custom-call(bf16[256,6144]{1,0:T(8,128)(2,1)} %get-tuple-element.9.y_in, bf16[256,128]{1,0:T(8,128)(2,1)} %get-tuple-element.10.k_in, bf16[256,128]{1,0:T(8,128)(2,1)} %get-tuple-element.11.v_in), custom_call_target="tpu_custom_call" | custom-call | tf_op jit(solution)/shard_map/copy_out/pallas_call | solution.py:560
  (1 shorter events, 0.0 us)

commit v7 on v6

--- a/solution.py
+++ b/solution.py
@@ -22,8 +22,9 @@
 BR = 8
 NBK, NBV = 4, 6
 TN = 512
-G_FINISH, G_PROJECT = 12, 13
-WO_FROM = 14
+G_FINISH, G_PROJECT = 10, 11
+G_TILE = 12
+WO_FROM = 8
 
 
 def rope_tables(positions, head_dim):
@@ -439,19 +440,20 @@
     def two_blocks_and_tile(g, _):
         two_blocks(g, 0)
 
-        @pl.when(g == last - 3)
+        @pl.when(g == G_TILE)
         def _():
             hid_copy.wait()
 
-        @pl.when(jnp.logical_or(g == last - 3, g == last - 1))
-        def _():
-            y_tile((g - (last - 3)) // 2)
+        @pl.when(jnp.logical_and(g >= G_TILE, (g - G_TILE) % 2 == 0))
+        def _():
+            y_tile((g - G_TILE) // 2)
         return 0
     lax.fori_loop(G_PROJECT, last, two_blocks_and_tile, 0)
     finish_part(1)
-    y_tile(2)
+    early = (last - G_TILE + 1) // 2
+    y_tile(early)
     project_part(1)
-    early = 3
+    early = early + 1
 
     def step(s, _):
         @pl.when(s + early < total)

time: 88.9 us -> 91.3 us (1.027)
  Pallas kernels: 86.2 us -> 88.5 us
    pallas_call x1, Pallas kernels: 83.4 us -> 85.7 us  [attention(): pl.pallas_call(attn_kernel, out_shape=[jax.ShapeDtypeStruct((n_rows, d_mo...]
where the time goes in v7:
time: 91.3 us; the launch traced here: 91.1 us
  Pallas kernels  88.5 us (97%)
  other arithmetic  1.94 us (2%)
    pallas_call x1, Pallas kernels, attention(): pl.pallas_call(attn_kernel, out_shape=[jax.ShapeDtypeStruct((n_rows, d_mo...  85.7 us
    pallas_call x1, Pallas kernels, copy_out(): pl.pallas_call(functools.partial(copy_kernel, parts), out_shape=[jax.Shap...  2.86 us

profile of v7, /device:TPU:0, one launch (start us, length us, event | category | flops | bytes accessed | tf_op | source)
XLA Modules:
  0.0 91.1 jit_solution(10243754685843052782)
XLA Ops:
  0.6 0.7 convert_element_type.10
  1.3 1.2 %fusion = (f32[256,128]{1,0:T(8,128)}, f32[256,128]{1,0:T(8,128)}) fusion(f32[128]{0:T(128)S(1)} %get-tuple-element.17, f32[128]{0:T(128)S(1)} %get-tuple-element.18, f32[256]{0:T(256)S(1)} %convert_element_type.10), kind=kLoop, calls=%fused_computation.2 | loop fusion | flops 65536 | bytes 264192 | tf_op jit(solution)/shard_map/mul | solution.py:37
  2.6 85.7 %attend.1 = (bf16[256,6144]{1,0:T(8,128)(2,1)}, bf16[256,128]{1,0:T(8,128)(2,1)}, bf16[256,128]{1,0:T(8,128)(2,1)}) custom-call(s32[256]{0:T(256)} %seq_ref.1, f32[256,128]{1,0:T(8,128)} %get-tuple-element.16.cos_ref, f32[256,128]{1,0:T(8,128)} %get-tuple-element.15.sin_ref, bf16[48,128]{1,0:T(8,128)(2,1)} %bitcast.10, bf16[24,128]{1,0:T(8,128)(2,1)} %bitcast.11, ...), custom_call_target="tpu_custom_call" | custom-call | tf_op jit(solution)/shard_map/attend/pallas_call | solution.py:505
  88.3 2.9 %copy_out.1 = (bf16[256,6144]{1,0:T(8,128)(2,1)}, bf16[256,128]{1,0:T(8,128)(2,1)}, bf16[256,128]{1,0:T(8,128)(2,1)}) custom-call(bf16[256,6144]{1,0:T(8,128)(2,1)} %get-tuple-element.9.y_in, bf16[256,128]{1,0:T(8,128)(2,1)} %get-tuple-element.10.k_in, bf16[256,128]{1,0:T(8,128)(2,1)} %get-tuple-element.11.v_in), custom_call_target="tpu_custom_call" | custom-call | tf_op jit(solution)/shard_map/copy_out/pallas_call | solution.py:562
  (1 shorter events, 0.0 us)

commit v8 on v6

--- a/solution.py
+++ b/solution.py
@@ -23,7 +23,6 @@
 NBK, NBV = 4, 6
 TN = 512
 G_FINISH, G_PROJECT = 12, 13
-WO_FROM = 14
 
 
 def rope_tables(positions, head_dim):
@@ -182,8 +181,11 @@
             q_ref[pl.ds(head, n_rows, stride=heads), :] = val
             q_send[t, pl.ds(h, n_rows, stride=tile_heads), :] = val
         q_copy(t).start()
+        wo_copy(2 * t).start()
+        wo_copy(2 * t + 1).start()
         return 0
     lax.fori_loop(0, n_q, q_tile, 0)
+    hid_copy.start()
 
     wk_copy.wait()
     wv_copy.wait()
@@ -333,16 +335,6 @@
         @pl.when(jnp.logical_and(b >= 2, b - 2 + NBV < n_blk))
         def _():
             v_copy(b - 2 + NBV).start()
-
-        w = b - WO_FROM
-
-        @pl.when(jnp.logical_and(w >= 0, jnp.logical_and(w % 2 == 0, w < 2 * n_tiles)))
-        def _():
-            wo_copy(w // 2).start()
-
-        @pl.when(w == 2 * n_tiles)
-        def _():
-            hid_copy.start()
 
         done = jnp.logical_and(b >= 2, (b - 2) % bq == bq - 1)
         u = b3 // bq

time: 88.9 us -> 89.5 us (level)
  no operation moved by 1% of the time
where the time goes in v8:
time: 89.5 us; the launch traced here: 89.4 us
  Pallas kernels  86.8 us (97%)
  other arithmetic  1.94 us (2%)
    pallas_call x1, Pallas kernels, attention(): pl.pallas_call(attn_kernel, out_shape=[jax.ShapeDtypeStruct((n_rows, d_mo...  83.9 us
    pallas_call x1, Pallas kernels, copy_out(): pl.pallas_call(functools.partial(copy_kernel, parts), out_shape=[jax.Shap...  2.86 us

profile of v8, /device:TPU:0, one launch (start us, length us, event | category | flops | bytes accessed | tf_op | source)
XLA Modules:
  0.0 89.4 jit_solution(15130873236185137643)
XLA Ops:
  0.6 0.7 convert_element_type.10
  1.3 1.2 %fusion = (f32[256,128]{1,0:T(8,128)}, f32[256,128]{1,0:T(8,128)}) fusion(f32[128]{0:T(128)S(1)} %get-tuple-element.17, f32[128]{0:T(128)S(1)} %get-tuple-element.18, f32[256]{0:T(256)S(1)} %convert_element_type.10), kind=kLoop, calls=%fused_computation.2 | loop fusion | flops 65536 | bytes 264192 | tf_op jit(solution)/shard_map/mul | solution.py:35
  2.6 83.9 %attend.1 = (bf16[256,6144]{1,0:T(8,128)(2,1)}, bf16[256,128]{1,0:T(8,128)(2,1)}, bf16[256,128]{1,0:T(8,128)(2,1)}) custom-call(s32[256]{0:T(256)} %seq_ref.1, f32[256,128]{1,0:T(8,128)} %get-tuple-element.16.cos_ref, f32[256,128]{1,0:T(8,128)} %get-tuple-element.15.sin_ref, bf16[48,128]{1,0:T(8,128)(2,1)} %bitcast.10, bf16[24,128]{1,0:T(8,128)(2,1)} %bitcast.11, ...), custom_call_target="tpu_custom_call" | custom-call | tf_op jit(solution)/shard_map/attend/pallas_call | solution.py:495
  86.5 2.9 %copy_out.1 = (bf16[256,6144]{1,0:T(8,128)(2,1)}, bf16[256,128]{1,0:T(8,128)(2,1)}, bf16[256,128]{1,0:T(8,128)(2,1)}) custom-call(bf16[256,6144]{1,0:T(8,128)(2,1)} %get-tuple-element.9.y_in, bf16[256,128]{1,0:T(8,128)(2,1)} %get-tuple-element.10.k_in, bf16[256,128]{1,0:T(8,128)(2,1)} %get-tuple-element.11.v_in), custom_call_target="tpu_custom_call" | custom-call | tf_op jit(solution)/shard_map/copy_out/pallas_call | solution.py:552
  (1 shorter events, 0.0 us)

commit v9 on v8

--- a/solution.py
+++ b/solution.py
@@ -22,6 +22,7 @@
 BR = 8
 NBK, NBV = 4, 6
 TN = 512
+TS = 256
 G_FINISH, G_PROJECT = 12, 13
 
 
@@ -224,9 +225,6 @@
             return acc
         new_sc[n] = lax.fori_loop(0, quarter // 8, rows8, zeros_q)
 
-    for n in range(NC):
-        new_scores(n)
-
     def column(vals, j):
         return jnp.broadcast_to(vals[:, j:j + 1], (heads, head_dim))
 
@@ -241,15 +239,13 @@
 
     def merge_core(u):
         k = u // 2
-        m1 = o_buf[u, o_rows:o_rows + heads, :]
-        l1 = o_buf[u, o_rows + heads:o_rows + 2 * heads, :]
-        m2 = rd[k, o_rows:o_rows + heads, :]
-        l2 = rd[k, o_rows + heads:o_rows + 2 * heads, :]
-        m = jnp.maximum(m1, m2)
-        f1 = jnp.exp2((m1 - m) * coef)
-        f2 = jnp.exp2((m2 - m) * coef)
-        o_buf[u, o_rows:o_rows + heads, :] = m
-        o_buf[u, o_rows + heads:o_rows + 2 * heads, :] = l1 * f1 + l2 * f2
+        st1 = o_buf[u, o_rows:o_rows + heads, :]
+        st2 = rd[k, o_rows:o_rows + heads, :]
+        m = jnp.maximum(st1, st2)
+        f1 = jnp.exp2((st1 - m) * coef)
+        f2 = jnp.exp2((st2 - m) * coef)
+        l = st1 * pltpu.roll(f1, quarter, 1) + st2 * pltpu.roll(f2, quarter, 1)
+        o_buf[u, o_rows:o_rows + heads, :] = jnp.where(lane < quarter, m, l)
 
         for j in range(quarter):
             rows = pl.ds(j * heads, heads)
@@ -258,16 +254,15 @@
     def finish(n):
         u = kept_group(n, 1)
         row0 = chip * chip_rows + n * 2 * quarter + core * quarter
-        m1 = o_buf[u, o_rows:o_rows + heads, :]
-        l1 = o_buf[u, o_rows + heads:o_rows + 2 * heads, :]
-        m2 = rx[n, o_rows:o_rows + heads, :]
-        l2 = rx[n, o_rows + heads:o_rows + 2 * heads, :]
+        st1 = o_buf[u, o_rows:o_rows + heads, :]
+        st2 = rx[n, o_rows:o_rows + heads, :]
         m3 = new_sc[n]
-        m = jnp.maximum(jnp.maximum(m1, m2), m3)
-        f1 = jnp.exp2((m1 - m) * coef)
-        f2 = jnp.exp2((m2 - m) * coef)
+        m = jnp.maximum(jnp.maximum(st1, st2), m3)
+        f1 = jnp.exp2((st1 - m) * coef)
+        f2 = jnp.exp2((st2 - m) * coef)
         f3 = jnp.exp2((m3 - m) * coef)
-        l = l1 * f1 + l2 * f2 + f3
+        l = st1 * pltpu.roll(f1, quarter, 1) + st2 * pltpu.roll(f2, quarter, 1) + pltpu.roll(f3, quarter, 1)
+        l = pltpu.roll(l, head_dim - quarter, 1)
         f1, f2, f3 = f1 / l, f2 / l, f3 / l
 
         for j in range(quarter):
@@ -292,8 +287,7 @@
             v_copy(b3).wait()
 
         u2, row2 = b2 // bq, block_row(b2)
-        m_all = o_buf[u2, o_rows:o_rows + heads, :]
-        l_all = o_buf[u2, o_rows + heads:o_rows + 2 * heads, :]
+        stats = o_buf[u2, o_rows:o_rows + heads, :]
         for pair in range(BR // 2):
             p_list = []
             for i in range(2):
@@ -303,13 +297,11 @@
                 m = jnp.maximum(jnp.max(s, axis=-1, keepdims=True), NEG_FLOOR)
                 p = jnp.exp2((s - m) * coef)
                 l = jnp.sum(p, axis=-1, keepdims=True)
-                here = lane == (b2 % bq) * BR + r
-                m_all = jnp.where(here, m, m_all)
-                l_all = jnp.where(here, l, l_all)
+                j = (b2 % bq) * BR + r
+                stats = jnp.where(lane == j, m, jnp.where(lane == quarter + j, l, stats))
                 p_list.append(p)
             p_sc[new, pair] = jnp.concatenate(p_list, axis=0).astype(jnp.bfloat16)
-        o_buf[u2, o_rows:o_rows + heads, :] = m_all
-        o_buf[u2, o_rows + heads:o_rows + 2 * heads, :] = l_all
+        o_buf[u2, o_rows:o_rows + heads, :] = stats
         row1, kslot = block_row(b1), b1 % NBK
         for pair in range(BR // 2):
             r = 2 * pair
@@ -369,6 +361,9 @@
     def yf_copy(i):
         return remote(y_chip.at[i], y_fwd.at[i], yf_s.at[i], yf_r.at[i], to_core)
 
+    per = TN // TS
+    n_sub = n_tiles * per
+
     def finish_part(h):
         for k in range(per_part):
             n = h * per_part + k
@@ -388,22 +383,28 @@
         def tile(t, _):
             if h == 0:
                 wo_copy(t).wait()
-            i = h * n_tiles + t
-            p_buf[i] = jnp.dot(lhs[...], wo[t], preferred_element_type=jnp.float32)
-            p_copy(i).start()
+            res = jnp.dot(lhs[...], wo[t], preferred_element_type=jnp.float32)
+            for k in range(per):
+                i = h * n_sub + t * per + k
+                p_buf[i] = res[:, k * TS:(k + 1) * TS]
+                p_copy(i).start()
+            if h == 1:
+                @pl.when(t % 2 == 1)
+                def _():
+                    y_tile(early + t // 2)
             return 0
         lax.fori_loop(0, n_tiles, tile, 0)
 
     def out_cols(i, on_core):
-        return pl.ds(pl.multiple_of(on_core * half + (i % n_tiles) * TN, TN), TN)
+        return pl.ds(pl.multiple_of(on_core * half + (i % n_sub) * TS, TS), TS)
 
     def out_rows(i, on_chip):
-        return pl.ds(pl.multiple_of(on_chip * chip_rows + (i // n_tiles) * part_rows, part_rows), part_rows)
+        return pl.ds(pl.multiple_of(on_chip * chip_rows + (i // n_sub) * part_rows, part_rows), part_rows)
 
     def y_tile(i):
         p_copy(i).wait_recv()
-        res = hid[pl.ds(pl.multiple_of((i // n_tiles) * part_rows, part_rows), part_rows),
-                  pl.ds(pl.multiple_of((i % n_tiles) * TN, TN), TN)].astype(jnp.float32)
+        res = hid[pl.ds(pl.multiple_of((i // n_sub) * part_rows, part_rows), part_rows),
+                  pl.ds(pl.multiple_of((i % n_sub) * TS, TS), TS)].astype(jnp.float32)
         y = (res + (p_buf[i] + p_recv[i])).astype(jnp.bfloat16)
         y_send[i] = y.astype(jnp.float32)
         y_ref[out_rows(i, chip), out_cols(i, core)] = y
@@ -421,29 +422,27 @@
         yf_copy(i).wait_recv()
         y_ref[out_rows(i, 1 - chip), out_cols(i, 1 - core)] = y_fwd[i].astype(jnp.bfloat16)
 
-    total = NH * n_tiles
+    total = NH * n_sub
     last = (n_blk + 2) // 2
     lax.fori_loop(0, G_FINISH, two_blocks, 0)
+    for n in range(NC):
+        new_scores(n)
     finish_part(0)
     lax.fori_loop(G_FINISH, G_PROJECT, two_blocks, 0)
+    early = last - G_PROJECT + 2
     project_part(0)
+    hid_copy.wait()
 
     def two_blocks_and_tile(g, _):
         two_blocks(g, 0)
-
-        @pl.when(g == last - 3)
-        def _():
-            hid_copy.wait()
-
-        @pl.when(jnp.logical_or(g == last - 3, g == last - 1))
-        def _():
-            y_tile((g - (last - 3)) // 2)
+        y_tile(g - G_PROJECT)
         return 0
     lax.fori_loop(G_PROJECT, last, two_blocks_and_tile, 0)
     finish_part(1)
-    y_tile(2)
+    y_tile(early - 2)
+    y_tile(early - 1)
     project_part(1)
-    early = 3
+    early = early + n_tiles // 2
 
     def step(s, _):
         @pl.when(s + early < total)
@@ -485,13 +484,13 @@
     n_tiles = half // TN
     n_q = w_q.shape[1] // (2 * TN)
     quarter = n_rows // (4 * NC)
-    msg = quarter * heads + 2 * heads
-    total = NH * n_tiles
+    msg = quarter * heads + heads
+    total = NH * n_tiles * (TN // TS)
     vmem = pl.BlockSpec(memory_space=pltpu.VMEM)
     hbm = pl.BlockSpec(memory_space=pl.ANY)
     f32, bf16 = jnp.float32, jnp.bfloat16
     dma = pltpu.SemaphoreType.DMA
-    tile_f32 = pltpu.VMEM((total, n_rows // (2 * NH), TN), f32)
+    tile_f32 = pltpu.VMEM((total, n_rows // (2 * NH), TS), f32)
     return pl.pallas_call(
         attn_kernel,
         out_shape=[jax.ShapeDtypeStruct((n_rows, d_model), bf16)] + [jax.ShapeDtypeStruct((n_rows, head_dim), bf16)] * 2,

time: 89.5 us -> 89.6 us (level)
  no operation moved by 1% of the time
where the time goes in v9:
time: 89.6 us; the launch traced here: 89.5 us
  Pallas kernels  86.9 us (97%)
  other arithmetic  1.94 us (2%)
    pallas_call x1, Pallas kernels, attention(): pl.pallas_call(attn_kernel, out_shape=[jax.ShapeDtypeStruct((n_rows, d_mo...  84.1 us
    pallas_call x1, Pallas kernels, copy_out(): pl.pallas_call(functools.partial(copy_kernel, parts), out_shape=[jax.Shap...  2.86 us

profile of v9, /device:TPU:0, one launch (start us, length us, event | category | flops | bytes accessed | tf_op | source)
XLA Modules:
  0.0 89.5 jit_solution(11773259137331991371)
XLA Ops:
  0.6 0.7 convert_element_type.10
  1.3 1.2 %fusion = (f32[256,128]{1,0:T(8,128)}, f32[256,128]{1,0:T(8,128)}) fusion(f32[128]{0:T(128)S(1)} %get-tuple-element.17, f32[128]{0:T(128)S(1)} %get-tuple-element.18, f32[256]{0:T(256)S(1)} %convert_element_type.10), kind=kLoop, calls=%fused_computation.2 | loop fusion | flops 65536 | bytes 264192 | tf_op jit(solution)/shard_map/mul | solution.py:36
  2.6 84.1 %attend.1 = (bf16[256,6144]{1,0:T(8,128)(2,1)}, bf16[256,128]{1,0:T(8,128)(2,1)}, bf16[256,128]{1,0:T(8,128)(2,1)}) custom-call(s32[256]{0:T(256)} %seq_ref.1, f32[256,128]{1,0:T(8,128)} %get-tuple-element.16.cos_ref, f32[256,128]{1,0:T(8,128)} %get-tuple-element.15.sin_ref, bf16[48,128]{1,0:T(8,128)(2,1)} %bitcast.10, bf16[24,128]{1,0:T(8,128)(2,1)} %bitcast.11, ...), custom_call_target="tpu_custom_call" | custom-call | tf_op jit(solution)/shard_map/attend/pallas_call | solution.py:494
  86.6 2.9 %copy_out.1 = (bf16[256,6144]{1,0:T(8,128)(2,1)}, bf16[256,128]{1,0:T(8,128)(2,1)}, bf16[256,128]{1,0:T(8,128)(2,1)}) custom-call(bf16[256,6144]{1,0:T(8,128)(2,1)} %get-tuple-element.9.y_in, bf16[256,128]{1,0:T(8,128)(2,1)} %get-tuple-element.10.k_in, bf16[256,128]{1,0:T(8,128)(2,1)} %get-tuple-element.11.v_in), custom_call_target="tpu_custom_call" | custom-call | tf_op jit(solution)/shard_map/copy_out/pallas_call | solution.py:551
  (1 shorter events, 0.0 us)

commit v10 on v9

--- a/solution.py
+++ b/solution.py
@@ -16,6 +16,7 @@
 VMEM_LIMIT = 67_043_328
 
 
+WO_FROM = 12
 NORM_ROWS = 32
 NC = 4
 NH = 2
@@ -182,11 +183,8 @@
             q_ref[pl.ds(head, n_rows, stride=heads), :] = val
             q_send[t, pl.ds(h, n_rows, stride=tile_heads), :] = val
         q_copy(t).start()
-        wo_copy(2 * t).start()
-        wo_copy(2 * t + 1).start()
         return 0
     lax.fori_loop(0, n_q, q_tile, 0)
-    hid_copy.start()
 
     wk_copy.wait()
     wv_copy.wait()
@@ -327,6 +325,16 @@
         @pl.when(jnp.logical_and(b >= 2, b - 2 + NBV < n_blk))
         def _():
             v_copy(b - 2 + NBV).start()
+
+        w = b - WO_FROM
+
+        @pl.when(jnp.logical_and(w >= 0, jnp.logical_and(w % 2 == 0, w < 2 * n_tiles)))
+        def _():
+            wo_copy(w // 2).start()
+
+        @pl.when(w == 0)
+        def _():
+            hid_copy.start()
 
         done = jnp.logical_and(b >= 2, (b - 2) % bq == bq - 1)
         u = b3 // bq

time: 89.6 us -> 88.8 us (level)
  no operation moved by 1% of the time
where the time goes in v10:
time: 88.8 us; the launch traced here: 88.7 us
  Pallas kernels  86.1 us (97%)
  other arithmetic  1.94 us (2%)
    pallas_call x1, Pallas kernels, attention(): pl.pallas_call(attn_kernel, out_shape=[jax.ShapeDtypeStruct((n_rows, d_mo...  83.3 us
    pallas_call x1, Pallas kernels, copy_out(): pl.pallas_call(functools.partial(copy_kernel, parts), out_shape=[jax.Shap...  2.86 us

profile of v10, /device:TPU:0, one launch (start us, length us, event | category | flops | bytes accessed | tf_op | source)
XLA Modules:
  0.0 88.7 jit_solution(7683183452229990185)
XLA Ops:
  0.6 0.7 convert_element_type.10
  1.3 1.2 %fusion = (f32[256,128]{1,0:T(8,128)}, f32[256,128]{1,0:T(8,128)}) fusion(f32[128]{0:T(128)S(1)} %get-tuple-element.17, f32[128]{0:T(128)S(1)} %get-tuple-element.18, f32[256]{0:T(256)S(1)} %convert_element_type.10), kind=kLoop, calls=%fused_computation.2 | loop fusion | flops 65536 | bytes 264192 | tf_op jit(solution)/shard_map/mul | solution.py:37
  2.6 83.3 %attend.1 = (bf16[256,6144]{1,0:T(8,128)(2,1)}, bf16[256,128]{1,0:T(8,128)(2,1)}, bf16[256,128]{1,0:T(8,128)(2,1)}) custom-call(s32[256]{0:T(256)} %seq_ref.1, f32[256,128]{1,0:T(8,128)} %get-tuple-element.16.cos_ref, f32[256,128]{1,0:T(8,128)} %get-tuple-element.15.sin_ref, bf16[48,128]{1,0:T(8,128)(2,1)} %bitcast.10, bf16[24,128]{1,0:T(8,128)(2,1)} %bitcast.11, ...), custom_call_target="tpu_custom_call" | custom-call | tf_op jit(solution)/shard_map/attend/pallas_call | solution.py:502
  85.8 2.9 %copy_out.1 = (bf16[256,6144]{1,0:T(8,128)(2,1)}, bf16[256,128]{1,0:T(8,128)(2,1)}, bf16[256,128]{1,0:T(8,128)(2,1)}) custom-call(bf16[256,6144]{1,0:T(8,128)(2,1)} %get-tuple-element.9.y_in, bf16[256,128]{1,0:T(8,128)(2,1)} %get-tuple-element.10.k_in, bf16[256,128]{1,0:T(8,128)(2,1)} %get-tuple-element.11.v_in), custom_call_target="tpu_custom_call" | custom-call | tf_op jit(solution)/shard_map/copy_out/pallas_call | solution.py:559
  (1 shorter events, 0.0 us)

commit v11 on v10

--- a/solution.py
+++ b/solution.py
@@ -21,7 +21,7 @@
 NC = 4
 NH = 2
 BR = 8
-NBK, NBV = 4, 6
+NBK, NBV = 6, 7
 TN = 512
 TS = 256
 G_FINISH, G_PROJECT = 12, 13
@@ -45,7 +45,7 @@
 
 def attn_kernel(seq_ref, cos_ref, sin_ref, nw_ref, bq_ref, bk_ref, bv_ref, hid_hbm, wq_hbm, wk_hbm, wv_hbm,
                 k_hbm, v_hbm, wo_hbm, y_ref, kb_ref, vb_ref,
-                q_ref, q_send, q_recv, wkv, bqf, kf_ref, vf_ref, in_sem, wkv_sem, q_s, q_r, o_buf, rd, rx, att, lhs, s_sc, p_sc, new_sc, p_buf, p_recv, y_send, y_core, y_chip, y_fwd, wo, hid,
+                q_ref, q_send, q_recv, bqf, kf_ref, vf_ref, in_sem, wkv_sem, q_s, q_r, o_buf, rd, rx, att, lhs, s_sc, p_sc, new_sc, p_buf, p_recv, y_send, y_core, y_chip, y_fwd, wo, hid,
                 kbuf, vbuf, k_sem, v_sem, wo_sem, hid_sem, rd_s, rd_r, rx_s, rx_r, at_s, at_r, p_s, p_r,
                 yc_s, yc_r, yx_s, yx_r, yf_s, yf_r):
     n_rows, d_model = y_ref.shape
@@ -114,8 +114,12 @@
         rows = pl.ds(pl.multiple_of(i * NORM_ROWS, NORM_ROWS), NORM_ROWS)
         return pltpu.make_async_copy(hid_hbm.at[rows], y_ref.at[rows], in_sem.at[i])
 
-    wk_copy = pltpu.make_async_copy(wk_hbm, wkv.at[:, :head_dim], wkv_sem.at[0])
-    wv_copy = pltpu.make_async_copy(wv_hbm, wkv.at[:, head_dim:], wkv_sem.at[1])
+
+    def wkv_copies():
+        parts = [(w, r) for r in range(2) for w in (wk_hbm, wv_hbm)]
+        return [pltpu.make_async_copy(w.at[pl.ds(r * k_half, k_half)],
+                                      wo.at[0, :, i * head_dim:(i + 1) * head_dim], wkv_sem.at[i])
+                for i, (w, r) in enumerate(parts)]
 
     def wq_copy(i):
         cols = pl.ds(pl.multiple_of((core * n_q + i // 2) * TN, TN), TN)
@@ -138,11 +142,6 @@
         @pl.when(i < 2 * n_q)
         def _():
             wq_copy(i).start()
-
-        @pl.when(i == n_norm - 1)
-        def _():
-            wk_copy.start()
-            wv_copy.start()
         sq = jnp.zeros((NORM_ROWS, 128), jnp.float32)
         for c in range(d_model // 128):
             x = y_ref[rows, c * 128:(c + 1) * 128].astype(jnp.float32)
@@ -183,12 +182,18 @@
             q_ref[pl.ds(head, n_rows, stride=heads), :] = val
             q_send[t, pl.ds(h, n_rows, stride=tile_heads), :] = val
         q_copy(t).start()
+
+        @pl.when(t == 0)
+        def _():
+            for c in wkv_copies():
+                c.start()
         return 0
     lax.fori_loop(0, n_q, q_tile, 0)
 
-    wk_copy.wait()
-    wv_copy.wait()
-    kv = jnp.dot(y_ref[...], wkv[...], preferred_element_type=jnp.float32)
+    for c in wkv_copies():
+        c.wait()
+    kv = jnp.dot(y_ref[:, :k_half], wo[0, :, :2 * head_dim], preferred_element_type=jnp.float32)
+    kv = kv + jnp.dot(y_ref[:, k_half:], wo[0, :, 2 * head_dim:], preferred_element_type=jnp.float32)
     k_rot = rope(round_f32(kv[:, :head_dim] + bk_ref[...].astype(jnp.float32)), cos_ref[...], sin_ref[...], even)
     kf_ref[...] = k_rot
     kb_ref[...] = k_rot.astype(jnp.bfloat16)
@@ -508,10 +513,9 @@
             pltpu.VMEM((n_rows * heads, head_dim), f32),
             pltpu.VMEM((n_q, n_rows * TN // head_dim, head_dim), f32),
             pltpu.VMEM((n_q, n_rows * TN // head_dim, head_dim), f32),
-            pltpu.VMEM((d_model, 2 * head_dim), bf16),
             pltpu.VMEM((heads, head_dim), f32),
             pltpu.VMEM((n_rows, head_dim), f32), pltpu.VMEM((n_rows, head_dim), f32),
-            dma((n_rows // NORM_ROWS,)), dma((2,)), dma((n_q,)), dma((n_q,)),
+            dma((n_rows // NORM_ROWS,)), dma((4,)), dma((n_q,)), dma((n_q,)),
             pltpu.VMEM((NC * 4, msg, head_dim), f32),
             pltpu.VMEM((NC * 2, msg, head_dim), f32),
             pltpu.VMEM((NC, msg, head_dim), f32),

time: 88.8 us -> 87.4 us (0.984)
  Pallas kernels: 86.1 us -> 84.6 us
    pallas_call x1, Pallas kernels: 83.3 us -> 81.8 us  [attention(): pl.pallas_call(attn_kernel, out_shape=[jax.ShapeDtypeStruct((n_rows, d_mo...]
where the time goes in v11:
time: 87.4 us; the launch traced here: 87.2 us
  Pallas kernels  84.6 us (97%)
  other arithmetic  1.94 us (2%)
    pallas_call x1, Pallas kernels, attention(): pl.pallas_call(attn_kernel, out_shape=[jax.ShapeDtypeStruct((n_rows, d_mo...  81.8 us
    pallas_call x1, Pallas kernels, copy_out(): pl.pallas_call(functools.partial(copy_kernel, parts), out_shape=[jax.Shap...  2.86 us

profile of v11, /device:TPU:0, one launch (start us, length us, event | category | flops | bytes accessed | tf_op | source)
XLA Modules:
  0.0 87.2 jit_solution(14611133898636780683)
XLA Ops:
  0.6 0.7 convert_element_type.10
  1.3 1.2 %fusion = (f32[256,128]{1,0:T(8,128)}, f32[256,128]{1,0:T(8,128)}) fusion(f32[128]{0:T(128)S(1)} %get-tuple-element.17, f32[128]{0:T(128)S(1)} %get-tuple-element.18, f32[256]{0:T(256)S(1)} %convert_element_type.10), kind=kLoop, calls=%fused_computation.2 | loop fusion | flops 65536 | bytes 264192 | tf_op jit(solution)/shard_map/mul | solution.py:37
  2.6 81.8 %attend.1 = (bf16[256,6144]{1,0:T(8,128)(2,1)}, bf16[256,128]{1,0:T(8,128)(2,1)}, bf16[256,128]{1,0:T(8,128)(2,1)}) custom-call(s32[256]{0:T(256)} %seq_ref.1, f32[256,128]{1,0:T(8,128)} %get-tuple-element.16.cos_ref, f32[256,128]{1,0:T(8,128)} %get-tuple-element.15.sin_ref, bf16[48,128]{1,0:T(8,128)(2,1)} %bitcast.10, bf16[24,128]{1,0:T(8,128)(2,1)} %bitcast.11, ...), custom_call_target="tpu_custom_call" | custom-call | tf_op jit(solution)/shard_map/attend/pallas_call | solution.py:507
  84.4 2.9 %copy_out.1 = (bf16[256,6144]{1,0:T(8,128)(2,1)}, bf16[256,128]{1,0:T(8,128)(2,1)}, bf16[256,128]{1,0:T(8,128)(2,1)}) custom-call(bf16[256,6144]{1,0:T(8,128)(2,1)} %get-tuple-element.9.y_in, bf16[256,128]{1,0:T(8,128)(2,1)} %get-tuple-element.10.k_in, bf16[256,128]{1,0:T(8,128)(2,1)} %get-tuple-element.11.v_in), custom_call_target="tpu_custom_call" | custom-call | tf_op jit(solution)/shard_map/copy_out/pallas_call | solution.py:563
  (1 shorter events, 0.0 us)

commit v12 on v11

--- a/solution.py
+++ b/solution.py
@@ -44,8 +44,8 @@
 
 
 def attn_kernel(seq_ref, cos_ref, sin_ref, nw_ref, bq_ref, bk_ref, bv_ref, hid_hbm, wq_hbm, wk_hbm, wv_hbm,
-                k_hbm, v_hbm, wo_hbm, y_ref, kb_ref, vb_ref,
-                q_ref, q_send, q_recv, bqf, kf_ref, vf_ref, in_sem, wkv_sem, q_s, q_r, o_buf, rd, rx, att, lhs, s_sc, p_sc, new_sc, p_buf, p_recv, y_send, y_core, y_chip, y_fwd, wo, hid,
+                k_hbm, v_hbm, wo_hbm, y_out, kb_ref, vb_ref,
+                y_ref, yo_sem, q_ref, q_send, q_recv, bqf, kf_ref, vf_ref, in_sem, wkv_sem, q_s, q_r, o_buf, rd, rx, att, lhs, s_sc, p_sc, new_sc, p_buf, p_recv, y_send, y_core, y_chip, y_fwd, wo, hid,
                 kbuf, vbuf, k_sem, v_sem, wo_sem, hid_sem, rd_s, rd_r, rx_s, rx_r, at_s, at_r, p_s, p_r,
                 yc_s, yc_r, yx_s, yx_r, yf_s, yf_r):
     n_rows, d_model = y_ref.shape
@@ -414,6 +414,10 @@
     def out_rows(i, on_chip):
         return pl.ds(pl.multiple_of(on_chip * chip_rows + (i // n_sub) * part_rows, part_rows), part_rows)
 
+    def out_copy(i, kind):
+        rows, cols = out_rows(i, (chip, 1 - chip)[kind % 2]), out_cols(i, (core, 1 - core)[kind // 2])
+        return pltpu.make_async_copy(y_ref.at[rows, cols], y_out.at[rows, cols], yo_sem.at[kind, i])
+
     def y_tile(i):
         p_copy(i).wait_recv()
         res = hid[pl.ds(pl.multiple_of((i // n_sub) * part_rows, part_rows), part_rows),
@@ -423,17 +427,21 @@
         y_ref[out_rows(i, chip), out_cols(i, core)] = y
         yx_copy(i).start()
         yc_copy(i).start()
+        out_copy(i, 0).start()
 
     def y_from_chip(i):
         yx_copy(i).wait_recv()
         yf_copy(i).start()
         y_ref[out_rows(i, 1 - chip), out_cols(i, core)] = y_chip[i].astype(jnp.bfloat16)
+        out_copy(i, 1).start()
         yc_copy(i).wait_recv()
         y_ref[out_rows(i, chip), out_cols(i, 1 - core)] = y_core[i].astype(jnp.bfloat16)
+        out_copy(i, 2).start()
 
     def y_from_fwd(i):
         yf_copy(i).wait_recv()
         y_ref[out_rows(i, 1 - chip), out_cols(i, 1 - core)] = y_fwd[i].astype(jnp.bfloat16)
+        out_copy(i, 3).start()
 
     total = NH * n_sub
     last = (n_blk + 2) // 2
@@ -485,6 +493,8 @@
         yc_copy(i).wait_send()
         yx_copy(i).wait_send()
         yf_copy(i).wait_send()
+        for kind in range(4):
+            out_copy(i, kind).wait()
         return 0
     lax.fori_loop(0, total, drain, 0)
 
@@ -508,8 +518,9 @@
         attn_kernel,
         out_shape=[jax.ShapeDtypeStruct((n_rows, d_model), bf16)] + [jax.ShapeDtypeStruct((n_rows, head_dim), bf16)] * 2,
         in_specs=[pl.BlockSpec(memory_space=pltpu.SMEM)] + [vmem] * 6 + [hbm] * 7,
-        out_specs=[vmem] * 3,
+        out_specs=[hbm, vmem, vmem],
         scratch_shapes=[
+            pltpu.VMEM((n_rows, d_model), bf16), dma((4, total)),
             pltpu.VMEM((n_rows * heads, head_dim), f32),
             pltpu.VMEM((n_q, n_rows * TN // head_dim, head_dim), f32),
             pltpu.VMEM((n_q, n_rows * TN // head_dim, head_dim), f32),

time: 87.4 us -> 87.4 us (level)
  no operation moved by 1% of the time
where the time goes in v12:
time: 87.4 us; the launch traced here: 87.3 us
  Pallas kernels  84.7 us (97%)
  other arithmetic  1.94 us (2%)
    pallas_call x1, Pallas kernels, attention(): pl.pallas_call(attn_kernel, out_shape=[jax.ShapeDtypeStruct((n_rows, d_mo...  81.8 us
    pallas_call x1, Pallas kernels, copy_out(): pl.pallas_call(functools.partial(copy_kernel, parts), out_shape=[jax.Shap...  2.86 us

profile of v12, /device:TPU:0, one launch (start us, length us, event | category | flops | bytes accessed | tf_op | source)
XLA Modules:
  0.0 87.3 jit_solution(12985228075208104757)
XLA Ops:
  0.6 0.7 convert_element_type.10
  1.3 1.2 %fusion = (f32[256,128]{1,0:T(8,128)}, f32[256,128]{1,0:T(8,128)}) fusion(f32[128]{0:T(128)S(1)} %get-tuple-element.17, f32[128]{0:T(128)S(1)} %get-tuple-element.18, f32[256]{0:T(256)S(1)} %convert_element_type.10), kind=kLoop, calls=%fused_computation.2 | loop fusion | flops 65536 | bytes 264192 | tf_op jit(solution)/shard_map/mul | solution.py:37
  2.6 81.8 %attend.1 = (bf16[256,6144]{1,0:T(8,128)(2,1)}, bf16[256,128]{1,0:T(8,128)(2,1)}, bf16[256,128]{1,0:T(8,128)(2,1)}) custom-call(s32[256]{0:T(256)} %seq_ref.1, f32[256,128]{1,0:T(8,128)} %get-tuple-element.16.cos_ref, f32[256,128]{1,0:T(8,128)} %get-tuple-element.15.sin_ref, bf16[48,128]{1,0:T(8,128)(2,1)} %bitcast.10, bf16[24,128]{1,0:T(8,128)(2,1)} %bitcast.11, ...), custom_call_target="tpu_custom_call" | custom-call | tf_op jit(solution)/shard_map/attend/pallas_call | solution.py:517
  84.4 2.9 %copy_out.1 = (bf16[256,6144]{1,0:T(8,128)(2,1)}, bf16[256,128]{1,0:T(8,128)(2,1)}, bf16[256,128]{1,0:T(8,128)(2,1)}) custom-call(bf16[256,6144]{1,0:T(8,128)(2,1)} %get-tuple-element.9.y_in, bf16[256,128]{1,0:T(8,128)(2,1)} %get-tuple-element.10.k_in, bf16[256,128]{1,0:T(8,128)(2,1)} %get-tuple-element.11.v_in), custom_call_target="tpu_custom_call" | custom-call | tf_op jit(solution)/shard_map/copy_out/pallas_call | solution.py:574
  (1 shorter events, 0.0 us)

commit v13 on v12

--- a/solution.py
+++ b/solution.py
@@ -21,7 +21,7 @@
 NC = 4
 NH = 2
 BR = 8
-NBK, NBV = 6, 7
+NBK, NBV = 6, 8
 TN = 512
 TS = 256
 G_FINISH, G_PROJECT = 12, 13
@@ -45,7 +45,7 @@
 
 def attn_kernel(seq_ref, cos_ref, sin_ref, nw_ref, bq_ref, bk_ref, bv_ref, hid_hbm, wq_hbm, wk_hbm, wv_hbm,
                 k_hbm, v_hbm, wo_hbm, y_out, kb_ref, vb_ref,
-                y_ref, yo_sem, q_ref, q_send, q_recv, bqf, kf_ref, vf_ref, in_sem, wkv_sem, q_s, q_r, o_buf, rd, rx, att, lhs, s_sc, p_sc, new_sc, p_buf, p_recv, y_send, y_core, y_chip, y_fwd, wo, hid,
+                y_ref, yo_sem, q_ref, q_send, q_recv, bqf, kf_ref, vf_ref, in_sem, wkv_sem, q_s, q_r, o_buf, rd, rx, att, lhs, s_sc, p_sc, new_sc, p_buf, p_recv, y_core, y_chip, y_fwd, wo, hid,
                 kbuf, vbuf, k_sem, v_sem, wo_sem, hid_sem, rd_s, rd_r, rx_s, rx_r, at_s, at_r, p_s, p_r,
                 yc_s, yc_r, yx_s, yx_r, yf_s, yf_r):
     n_rows, d_model = y_ref.shape
@@ -366,10 +366,10 @@
         return remote(p_buf.at[i], p_recv.at[i], p_s.at[i], p_r.at[i], to_tp)
 
     def yc_copy(i):
-        return remote(y_send.at[i], y_core.at[i], yc_s.at[i], yc_r.at[i], to_core)
+        return remote(p_buf.at[i], y_core.at[i], yc_s.at[i], yc_r.at[i], to_core)
 
     def yx_copy(i):
-        return remote(y_send.at[i], y_chip.at[i], yx_s.at[i], yx_r.at[i], to_chip)
+        return remote(p_buf.at[i], y_chip.at[i], yx_s.at[i], yx_r.at[i], to_chip)
 
     def yf_copy(i):
         return remote(y_chip.at[i], y_fwd.at[i], yf_s.at[i], yf_r.at[i], to_core)
@@ -423,7 +423,8 @@
         res = hid[pl.ds(pl.multiple_of((i // n_sub) * part_rows, part_rows), part_rows),
                   pl.ds(pl.multiple_of((i % n_sub) * TS, TS), TS)].astype(jnp.float32)
         y = (res + (p_buf[i] + p_recv[i])).astype(jnp.bfloat16)
-        y_send[i] = y.astype(jnp.float32)
+        p_copy(i).wait_send()
+        p_buf[i] = y.astype(jnp.float32)
         y_ref[out_rows(i, chip), out_cols(i, core)] = y
         yx_copy(i).start()
         yc_copy(i).start()
@@ -489,7 +490,6 @@
         at_copy(n).wait_send()
 
     def drain(i, _):
-        p_copy(i).wait_send()
         yc_copy(i).wait_send()
         yx_copy(i).wait_send()
         yf_copy(i).wait_send()
@@ -535,7 +535,7 @@
             pltpu.VMEM((2, BR // 2, 2 * heads, s_dev), f32),
             pltpu.VMEM((2, BR // 2, 2 * heads, s_dev), bf16),
             pltpu.VMEM((NC, heads, head_dim), f32),
-            tile_f32, tile_f32, tile_f32, tile_f32, tile_f32, tile_f32,
+            tile_f32, tile_f32, tile_f32, tile_f32, tile_f32,
             pltpu.VMEM((n_tiles, heads * head_dim, TN), bf16),
             pltpu.VMEM((n_rows // 2, half), bf16),
             pltpu.VMEM((NBK, BR, s_dev, head_dim), bf16),

time: 87.4 us -> 87.1 us (level)
  no operation moved by 1% of the time
where the time goes in v13:
time: 87.1 us; the launch traced here: 86.9 us
  Pallas kernels  84.3 us (97%)
  other arithmetic  1.94 us (2%)
    pallas_call x1, Pallas kernels, attention(): pl.pallas_call(attn_kernel, out_shape=[jax.ShapeDtypeStruct((n_rows, d_mo...  81.5 us
    pallas_call x1, Pallas kernels, copy_out(): pl.pallas_call(functools.partial(copy_kernel, parts), out_shape=[jax.Shap...  2.86 us

profile of v13, /device:TPU:0, one launch (start us, length us, event | category | flops | bytes accessed | tf_op | source)
XLA Modules:
  0.0 86.9 jit_solution(11246930896987632603)
XLA Ops:
  0.6 0.7 convert_element_type.10
  1.3 1.2 %fusion = (f32[256,128]{1,0:T(8,128)}, f32[256,128]{1,0:T(8,128)}) fusion(f32[128]{0:T(128)S(1)} %get-tuple-element.17, f32[128]{0:T(128)S(1)} %get-tuple-element.18, f32[256]{0:T(256)S(1)} %convert_element_type.10), kind=kLoop, calls=%fused_computation.2 | loop fusion | flops 65536 | bytes 264192 | tf_op jit(solution)/shard_map/mul | solution.py:37
  2.6 81.5 %attend.1 = (bf16[256,6144]{1,0:T(8,128)(2,1)}, bf16[256,128]{1,0:T(8,128)(2,1)}, bf16[256,128]{1,0:T(8,128)(2,1)}) custom-call(s32[256]{0:T(256)} %seq_ref.1, f32[256,128]{1,0:T(8,128)} %get-tuple-element.16.cos_ref, f32[256,128]{1,0:T(8,128)} %get-tuple-element.15.sin_ref, bf16[48,128]{1,0:T(8,128)(2,1)} %bitcast.10, bf16[24,128]{1,0:T(8,128)(2,1)} %bitcast.11, ...), custom_call_target="tpu_custom_call" | custom-call | tf_op jit(solution)/shard_map/attend/pallas_call | solution.py:517
  84.0 2.9 %copy_out.1 = (bf16[256,6144]{1,0:T(8,128)(2,1)}, bf16[256,128]{1,0:T(8,128)(2,1)}, bf16[256,128]{1,0:T(8,128)(2,1)}) custom-call(bf16[256,6144]{1,0:T(8,128)(2,1)} %get-tuple-element.9.y_in, bf16[256,128]{1,0:T(8,128)(2,1)} %get-tuple-element.10.k_in, bf16[256,128]{1,0:T(8,128)(2,1)} %get-tuple-element.11.v_in), custom_call_target="tpu_custom_call" | custom-call | tf_op jit(solution)/shard_map/copy_out/pallas_call | solution.py:574
  (1 shorter events, 0.0 us)
